TPU v7x, 64 devices: a 2x2x8 block of a 4x4x8 slice. The times are simulated.
64 devices in a mesh: dp: 4 (over x, y), tp: 16 (over z, core).
Axes of the slice: x: 2, y: 2, z: 8, core: 2. Of those that a mesh axis runs over, the one named last changes fastest.
The devices are a block of a 4x4x8 slice.
Arguments:
- x: bfloat16 [8, 1024, 2048], P('dp', 'tp'), parts along dimension 0
- k_cache: bfloat16 [8, 8192, 16, 128], P('dp', None, 'tp'), parts along dimension 0
- v_cache: bfloat16 [8, 8192, 16, 128], P('dp', None, 'tp'), parts along dimension 0
- prefix_len: int32 [8], P('dp'), parts along dimension 0
- valid_len: int32 [8], P('dp'), parts along dimension 0
- g_attn: bfloat16 [2048], replicated
- w_q: bfloat16 [2048, 2048], P(None, 'tp')
- b_q: bfloat16 [2048], P('tp')
- w_k: bfloat16 [2048, 2048], P(None, 'tp')
- b_k: bfloat16 [2048], P('tp')
- w_v: bfloat16 [2048, 2048], P(None, 'tp')
- b_v: bfloat16 [2048], P('tp')
- w_o: bfloat16 [2048, 2048], P('tp')
- g_mlp: bfloat16 [2048], replicated
- w_gate: bfloat16 [2048, 11008], P(None, 'tp')
- w_up: bfloat16 [2048, 11008], P(None, 'tp')
- w_down: bfloat16 [11008, 2048], P('tp')
Outputs:
- output 1: bfloat16 [8, 1024, 2048], P('dp', 'tp'), parts along dimension 0
- output 2: bfloat16 [8, 8192, 16, 128], P('dp', None, 'tp'), parts along dimension 0
- output 3: bfloat16 [8, 8192, 16, 128], P('dp', None, 'tp'), parts along dimension 0
There are 4 independent parts. A program takes and returns all parts, laid end to end along the dimension named above; an argument that names none is the same for every part.
All inputs are finite; a program needn't handle non-finite values.
Results may differ from a plain program's by a relative error of at most 0.02.
Values are sent between devices in bfloat16 or wider.
A program may use at most 768 MiB of HBM per device.

v0:
```python
import jax
import jax.numpy as jnp
from jax import lax
from jax.sharding import PartitionSpec as P

ROPE_THETA = 1.0e6
NORM_EPS = 1.0e-6


def rms_norm(hidden, gain):
    wide_vals = hidden.astype(jnp.float32)
    inv_rms = lax.rsqrt(jnp.mean(wide_vals * wide_vals, axis=-1, keepdims=True) + NORM_EPS)
    return (wide_vals * inv_rms * gain.astype(jnp.float32)).astype(jnp.bfloat16)


def rotate_heads(heads, positions):
    half = heads.shape[-1] // 2
    inv_freq = ROPE_THETA ** (-(jnp.arange(half, dtype=jnp.float32) * 2.0) / heads.shape[-1])
    angles = positions.astype(jnp.float32)[..., None] * inv_freq
    cos_t = jnp.cos(angles)[..., None, :]
    sin_t = jnp.sin(angles)[..., None, :]
    wide = heads.astype(jnp.float32)
    first_half = wide[..., :half]
    second_half = wide[..., half:]
    rotated = jnp.concatenate([first_half * cos_t - second_half * sin_t, second_half * cos_t + first_half * sin_t], axis=-1)
    return rotated.astype(jnp.bfloat16)


def project(hidden, weight, bias):
    total = jnp.einsum("rcd,dn->rcn", hidden, weight, preferred_element_type=jnp.float32)
    return (total + bias.astype(jnp.float32)).astype(jnp.bfloat16)


def write_rows(cache, new_rows, prefix, valid):
    n_tokens = new_rows.shape[1]
    row_ids = jnp.arange(n_tokens, dtype=jnp.int32)[None, :, None, None]
    window = (1, n_tokens, cache.shape[2], cache.shape[3])

    def body(req_idx, buffer):
        start = prefix[req_idx]
        old_rows = lax.dynamic_slice(buffer, (req_idx, start, 0, 0), window)
        fresh = lax.dynamic_slice_in_dim(new_rows, req_idx, 1, axis=0)
        merged = jnp.where(row_ids < valid[req_idx], fresh, old_rows)
        return lax.dynamic_update_slice(buffer, merged, (req_idx, start, 0, 0))

    return lax.fori_loop(0, cache.shape[0], body, cache)


def attend(queries, k_cache, v_cache, prefix, valid):
    n_req, n_tokens, q_heads, head_dim = queries.shape
    slots, kv_local = k_cache.shape[1], k_cache.shape[2]
    query_groups = queries.reshape(n_req, n_tokens, kv_local, q_heads // kv_local, head_dim)
    scores = jnp.einsum("rckgd,rskd->rkgcs", query_groups, k_cache, preferred_element_type=jnp.float32) * (head_dim ** -0.5)
    row_ids = jnp.arange(n_tokens, dtype=jnp.int32)
    limit = prefix[:, None] + jnp.minimum(row_ids[None, :], valid[:, None] - 1)
    visible = jnp.arange(slots, dtype=jnp.int32)[None, None, :] <= limit[:, :, None]
    scores = jnp.where(visible[:, None, None], scores, -1.0e30)
    attn_probs = jax.nn.softmax(scores, axis=-1).astype(jnp.bfloat16)
    mixed = jnp.einsum("rkgcs,rskd->rckgd", attn_probs, v_cache, preferred_element_type=jnp.float32)
    return mixed.astype(jnp.bfloat16).reshape(n_req, n_tokens, q_heads * head_dim)


def attention_heads(normed_full, k_cache, v_cache, prefix, valid, w_q, b_q, w_k, b_k, w_v, b_v):
    n_req, n_tokens = normed_full.shape[0], normed_full.shape[1]
    head_dim = k_cache.shape[-1]
    positions = prefix[:, None] + jnp.arange(n_tokens, dtype=jnp.int32)[None, :]
    queries = rotate_heads(project(normed_full, w_q, b_q).reshape(n_req, n_tokens, -1, head_dim), positions)
    keys_new = rotate_heads(project(normed_full, w_k, b_k).reshape(n_req, n_tokens, -1, head_dim), positions)
    values_new = project(normed_full, w_v, b_v).reshape(n_req, n_tokens, -1, head_dim)
    k_out = write_rows(k_cache, keys_new, prefix, valid)
    v_out = write_rows(v_cache, values_new, prefix, valid)
    return attend(queries, k_out, v_out, prefix, valid), k_out, v_out


def mlp_partial(normed_full, w_gate, w_up, w_down):
    gate = jnp.einsum("rcd,df->rcf", normed_full, w_gate, preferred_element_type=jnp.float32)
    up_proj = jnp.einsum("rcd,df->rcf", normed_full, w_up, preferred_element_type=jnp.float32)
    hidden_act = (jax.nn.silu(gate) * up_proj).astype(jnp.bfloat16)
    return jnp.einsum("rcf,fd->rcd", hidden_act, w_down, preferred_element_type=jnp.float32).astype(jnp.bfloat16)


def add_rounded(first, second):
    return (first.astype(jnp.float32) + second.astype(jnp.float32)).astype(jnp.bfloat16)


def solution(mesh):
    row_spec = P("dp", "tp", None)
    cache_spec = P("dp", None, "tp", None)
    req_spec = P("dp")
    rep_spec = P(None)
    col_spec = P(None, "tp")
    bias_spec = P("tp")
    down_spec = P("tp", None)

    def layer(x_rows, k_cache, v_cache, prefix, valid, g_attn, w_q, b_q, w_k, b_k, w_v, b_v, w_o, g_mlp, w_gate, w_up, w_down):
        normed = rms_norm(x_rows, g_attn)
        normed_full = lax.all_gather(normed, "tp", axis=1, tiled=True)
        attended, k_out, v_out = attention_heads(normed_full, k_cache, v_cache, prefix, valid, w_q, b_q, w_k, b_k, w_v, b_v)
        attn_part = jnp.einsum("rcn,nd->rcd", attended, w_o, preferred_element_type=jnp.float32).astype(jnp.bfloat16)
        attn_rows = lax.psum_scatter(attn_part, "tp", scatter_dimension=1, tiled=True)
        resid_mid = add_rounded(x_rows, attn_rows)
        normed_mlp = rms_norm(resid_mid, g_mlp)
        mlp_full = lax.all_gather(normed_mlp, "tp", axis=1, tiled=True)
        down_part = mlp_partial(mlp_full, w_gate, w_up, w_down)
        down_rows = lax.psum_scatter(down_part, "tp", scatter_dimension=1, tiled=True)
        return add_rounded(resid_mid, down_rows), k_out, v_out

    in_specs = (row_spec, cache_spec, cache_spec, req_spec, req_spec, rep_spec, col_spec, bias_spec, col_spec, bias_spec, col_spec, bias_spec, down_spec, rep_spec, col_spec, col_spec, down_spec)
    return jax.shard_map(layer, mesh=mesh, in_specs=in_specs, out_specs=(row_spec, cache_spec, cache_spec), check_vma=False)
```

profile of v0, /device:TPU:28, one launch (start us, length us, event | category | flops | bytes accessed | tf_op | source)
XLA Modules:
  0.0 431.3 jit_solution(4453522219611948031)
XLA Ops:
  7.3 4.8 %copy.63 = bf16[2,8192,1,128]{3,1,2,0:T(8,128)(2,1)} copy(bf16[2,8192,1,128]{3,1,2,0:T(8,128)(2,1)} %param.22) | data formatting | bytes 8388608
  12.1 2.0 copy.64
  15.6 55.9 %all-gather.3.cloned.1.call-done = bf16[2,1024,2048]{2,1,0:T(8,128)(2,1)} async-done(((bf16[2,64,2048]{2,1,0:T(8,128)(2,1)}), bf16[2,1024,2048]{2,1,0:T(8,128)(2,1)}) %all-gather.3.cloned.1.call-update) | async-done | bytes 8388624 | tf_op jit(solution)/shard_map/all_gather | solution.py:97
  71.6 6.5 %fusion.24 = f32[2,1024,1,128]{1,3,0,2:T(8,128)S(1)} fusion(bf16[2,1024,2048]{2,1,0:T(8,128)(2,1)} %all-gather.3.cloned.1.call-done, bf16[2048,128]{1,0:T(8,128)(2,1)} %param.27, f32[128]{0:T(128)S(1)} %convert_element_type.115), kind=kOutput, calls=%fused_computation.39 | convolution fusion | flops 1074528256 | bytes 9961984 | tf_op jit(solution)/shard_map/rcd,dn->rcn/dot_general | solution.py:30
  78.1 3.9 fusion.26
  82.0 3.3 fusion.71
  86.2 16.0 %while.29 = (s32[]{:T(128)}, bf16[2,8192,1,128]{3,1,2,0:T(8,128)(2,1)}, s32[2]{0:T(128)S(1)}, bf16[2,1024,1,128]{1,3,0,2:T(8,128)(2,1)}, s32[2]{0:T(128)S(1)}, /*index=5*/s32[]{:T(128)}, s32[]{:T(128)}, s32[]{:T(128)}) while((s32[]{:T(128)}, bf16[2,8192,1,128]{3,1,2,0:T(8,128)(2,1)}, s32[2]{0:T(128)S(1)}, ...), condition=%wide.region_4.5_spmd.clone, body=%wide.region_3.4_spmd.clone.sunk | while | flops 132101 | bytes 2361507 | solution.py:46
  91.9 2.7 dynamic_update_slice.19
  100.4 1.8 dynamic_update_slice.19
  102.2 6.6 %fusion.27 = bf16[2,1024,1,128]{3,1,2,0:T(8,128)(2,1)} fusion(bf16[2,1024,2048]{2,1,0:T(8,128)(2,1)} %all-gather.3.cloned.1.call-done, bf16[2048,128]{1,0:T(8,128)(2,1)} %param.31, f32[128]{0:T(128)S(1)} %convert_element_type.108), kind=kOutput, calls=%fused_computation.42 | convolution fusion | flops 1074266112 | bytes 9437696 | tf_op jit(solution)/shard_map/rcd,dn->rcn/dot_general | solution.py:30
  108.8 15.3 %while.28 = (s32[]{:T(128)}, bf16[2,8192,1,128]{3,1,2,0:T(8,128)(2,1)}, s32[2]{0:T(128)S(1)}, bf16[2,1024,1,128]{3,1,2,0:T(8,128)(2,1)}, s32[2]{0:T(128)S(1)}, /*index=5*/s32[]{:T(128)}, s32[]{:T(128)}, s32[]{:T(128)}) while((s32[]{:T(128)}, bf16[2,8192,1,128]{3,1,2,0:T(8,128)(2,1)}, s32[2]{0:T(128)S(1)}, ...), condition=%wide.region_2.3_spmd.clone, body=%wide.region_1.2_spmd.clone.sunk | while | flops 132101 | bytes 1312927 | solution.py:46
  114.2 2.7 dynamic_update_slice.18
  122.3 1.8 dynamic_update_slice.18
  124.1 26.6 %fusion.5 = (f32[2,1024]{1,0:T(2,128)S(1)}, f32[2,8192,1024]{2,1,0:T(8,128)}) fusion(s32[2,1024]{1,0:T(2,128)S(1)} %get-tuple-element.293, bf16[2,1024,64]{1,2,0:T(8,128)(2,1)} %get-tuple-element.288, bf16[2,1024,64]{1,2,0:T(8,128)(2,1)S(1)} %copy-done.5, bf16[2,8192,1,128]{3,1,2,0:T(8,128)(2,1)} %get-tuple-element.219), kind=kOutput, calls=%fused_computation.12 | convolution fusion | flops 4363122688 | bytes 71843840 | tf_op jit(solution)/shard_map/rckgd,rskd->rkgcs/dot_general | solution.py:53
  150.7 21.8 %fusion.4 = f32[2,1024]{1,0:T(2,128)S(1)} fusion(f32[2,8192,1024]{2,1,0:T(8,128)} %get-tuple-element.296, f32[2,1024]{1,0:T(2,128)S(1)} %get-tuple-element.295, s32[2,1024]{1,0:T(2,128)S(1)} %get-tuple-element.293), kind=kLoop, calls=%fused_computation.11 | loop fusion | flops 83884032 | bytes 67133440 | tf_op jit(solution)/shard_map/reduce_sum | solution.py:58
  172.5 32.3 %convolution_convert_fusion.1 = bf16[2,1024,2048]{2,1,0:T(8,128)(2,1)} fusion(f32[2,1024]{1,0:T(2,128)S(1)} %fusion.4, f32[2,1024]{1,0:T(2,128)S(1)} %get-tuple-element.295, f32[2,8192,1024]{2,1,0:T(8,128)} %get-tuple-element.296, s32[2,1024]{1,0:T(2,128)S(1)} %get-tuple-element.293, bf16[2,8192,1,128]{3,1,2,0:T(8,128)(2,1)} %get-tuple-element.220, ...), kind=kOutput, calls=%fused_computation.17 | convolution fusion | flops 5473828864 | bytes 80240640 | tf_op jit(solution)/shard_map/rcn,nd->rcd/dot_general | solution.py:99
  205.5 65.4 %reduce-scatter.3.cloned.1.call-done = bf16[2,64,2048]{2,1,0:T(8,128)(2,1)} async-done(((bf16[2,1024,2048]{2,1,0:T(8,128)(2,1)}), bf16[2,64,2048]{2,1,0:T(8,128)(2,1)}) %reduce-scatter.3.cloned.1.call-update) | async-done | bytes 524304 | tf_op jit(solution)/shard_map/reduce_scatter | solution.py:100
  270.9 1.3 fusion.41
  272.2 2.0 fusion.43
  274.4 51.6 %all-gather.5.cloned.1.call-done = bf16[2,1024,2048]{2,1,0:T(8,128)(2,1)} async-done(((bf16[2,64,2048]{2,1,0:T(8,128)(2,1)}), bf16[2,1024,2048]{2,1,0:T(8,128)(2,1)}) %all-gather.5.cloned.1.call-update) | async-done | bytes 8388624 | tf_op jit(solution)/shard_map/all_gather | solution.py:103
  326.0 10.9 %fusion.12 = f32[2,1024,688]{1,2,0:T(8,128)} fusion(bf16[2,1024,2048]{2,1,0:T(8,128)(2,1)} %all-gather.5.cloned.1.call-done, bf16[2048,688]{0,1:T(8,128)(2,1)} %param.36), kind=kOutput, calls=%fused_computation.22 | convolution fusion | flops 5771362304 | bytes 16842752 | tf_op jit(solution)/shard_map/rcd,df->rcf/dot_general | solution.py:77
  336.9 19.3 %convolution_convert_fusion = bf16[2,1024,2048]{2,1,0:T(8,128)(2,1)} fusion(bf16[688,2048]{1,0:T(8,128)(2,1)S(1)} %copy-done, f32[2,1024,688]{1,2,0:T(8,128)} %fusion.12, bf16[2,1024,2048]{2,1,0:T(8,128)(2,1)} %all-gather.5.cloned.1.call-done, bf16[2048,688]{0,1:T(8,128)(2,1)} %param.35), kind=kOutput, calls=%fused_computation.16 | convolution fusion | flops 11555373056 | bytes 28049408 | tf_op jit(solution)/shard_map/rcf,fd->rcd/dot_general | solution.py:79
  356.2 66.3 %reduce-scatter.5.cloned.1.call-done = bf16[2,64,2048]{2,1,0:T(8,128)(2,1)} async-done(((bf16[2,1024,2048]{2,1,0:T(8,128)(2,1)}), bf16[2,64,2048]{2,1,0:T(8,128)(2,1)}) %reduce-scatter.5.cloned.1.call-update) | async-done | bytes 524304 | tf_op jit(solution)/shard_map/reduce_scatter | solution.py:105
  422.5 2.2 fusion.44
  (67 shorter events, 17.9 us)
Async XLA Ops:
  7.2 329.7 %copy-start = (bf16[688,2048]{1,0:T(8,128)(2,1)S(1)}, bf16[688,2048]{1,0:T(8,128)(2,1)}, u32[]{:S(2)}) copy-start(bf16[688,2048]{1,0:T(8,128)(2,1)} %param.37) | copy-start | bytes 8454148
  7.2 6.9 %copy-start.2 = (bf16[2,64,2048]{2,1,0:T(8,128)(2,1)S(1)}, bf16[2,64,2048]{2,1,0:T(8,128)(2,1)}, u32[]{:S(2)}) copy-start(bf16[2,64,2048]{2,1,0:T(8,128)(2,1)} %param.21) | copy-start | bytes 1572868
  7.2 8.3 %copy-start.8 = (s32[2]{0:T(128)S(1)}, s32[2]{0:T(128)}, u32[]{:S(2)}) copy-start(s32[2]{0:T(128)} %param.24) | copy-start | bytes 28
  7.2 8.3 %copy-start.12 = (s32[2]{0:T(128)S(1)}, s32[2]{0:T(128)}, u32[]{:S(2)}) copy-start(s32[2]{0:T(128)} %param.25) | copy-start | bytes 28
  7.2 6.9 %copy-start.6 = (bf16[2048]{0:T(1024)(128)(2,1)S(1)}, bf16[2048]{0:T(1024)(128)(2,1)}, u32[]{:S(2)}) copy-start(bf16[2048]{0:T(1024)(128)(2,1)} %param.26) | copy-start | bytes 12292
  7.2 8.2 %copy-start.9 = (bf16[128]{0:T(256)(128)(2,1)S(1)}, bf16[128]{0:T(256)(128)(2,1)}, u32[]{:S(2)}) copy-start(bf16[128]{0:T(256)(128)(2,1)} %param.28) | copy-start | bytes 772
  7.2 8.2 %copy-start.10 = (bf16[128]{0:T(256)(128)(2,1)S(1)}, bf16[128]{0:T(256)(128)(2,1)}, u32[]{:S(2)}) copy-start(bf16[128]{0:T(256)(128)(2,1)} %param.30) | copy-start | bytes 772
  7.3 8.2 %copy-start.11 = (bf16[128]{0:T(256)(128)(2,1)S(1)}, bf16[128]{0:T(256)(128)(2,1)}, u32[]{:S(2)}) copy-start(bf16[128]{0:T(256)(128)(2,1)} %param.32) | copy-start | bytes 772
  7.3 64.3 %all-gather.3.cloned.1.call-start = ((), (), s32[]{:S(2)}) async-start(), calls=%async_computation.2 | async-start | bytes 8912896 | tf_op jit(solution)/shard_map/all_gather | solution.py:97
  7.3 4.8 %copy-start.4 = (bf16[2,8192,1,128]{3,1,2,0:T(8,128)(2,1)S(1)}, bf16[2,8192,1,128]{3,1,2,0:T(8,128)(2,1)}, u32[]{:S(2)}) copy-start(bf16[2,8192,1,128]{3,1,2,0:T(8,128)(2,1)} %param.23) | copy-start | bytes 12582916
  15.4 255.5 %reduce-scatter.3.cloned.1.call-start = ((), (), s32[]{:S(2)}) async-start(), calls=%async_computation.3 | async-start | bytes 8912896 | tf_op jit(solution)/shard_map/reduce_scatter | solution.py:100
  71.6 6.5 %copy-start.1 = (bf16[2,1024,2048]{2,1,0:T(8,128)(2,1)S(1)}, bf16[2,1024,2048]{2,1,0:T(8,128)(2,1)}, u32[]{:S(2)}) copy-start(bf16[2,1024,2048]{2,1,0:T(8,128)(2,1)} %all-gather.3.cloned.1.call-done) | copy-start | bytes 25165828
  102.2 21.9 %copy-start.5 = (bf16[2,1024,64]{1,2,0:T(8,128)(2,1)S(1)}, bf16[2,1024,64]{1,2,0:T(8,128)(2,1)}, u32[]{:S(2)}) copy-start(bf16[2,1024,64]{1,2,0:T(8,128)(2,1)} %get-tuple-element.287) | copy-start | bytes 786436
  204.8 0.7 copy-start.7
  204.8 66.1 %copy-start.3 = (bf16[2,64,2048]{2,1,0:T(8,128)(2,1)S(1)}, bf16[2,64,2048]{2,1,0:T(8,128)(2,1)}, u32[]{:S(2)}) copy-start(bf16[2,64,2048]{2,1,0:T(8,128)(2,1)} %param.21) | copy-start | bytes 1572868
  204.8 121.1 %all-gather.5.cloned.1.call-start = ((), (), s32[]{:S(2)}) async-start(), calls=%async_computation.4 | async-start | bytes 8912896 | tf_op jit(solution)/shard_map/all_gather | solution.py:103
  274.3 148.2 %reduce-scatter.5.cloned.1.call-start = ((), (), s32[]{:S(2)}) async-start(), calls=%async_computation.5 | async-start | bytes 8912896 | tf_op jit(solution)/shard_map/reduce_scatter | solution.py:105
Sparse Core Ops, SparseCore 0:
  15.5 56.0 all-gather.2
  205.0 65.9 reduce-scatter.2
  274.5 51.4 all-gather.4
  356.3 66.1 reduce-scatter.4
where the time goes:
time: 432 us; the launch traced here: 431 us
  waiting for transfers between devices  239 us (55%)
  matrix products  106 us (25%)
  other arithmetic  40.2 us (9%)
  local copies, waits for them, and re-layouts  23.7 us (5%)
  between operations  14 us (3%)
  loops' own time  7.57 us (2%)
    reduce_scatter x1, waiting for transfers between devices, layer(): lax.psum_scatter(down_part, 'tp', scatter_dimension=1, tiled=True)  66.3 us
    reduce_scatter x1, waiting for transfers between devices, layer(): lax.psum_scatter(attn_part, 'tp', scatter_dimension=1, tiled=True)  65.4 us
    all_gather x1, waiting for transfers between devices, layer(): normed_full = lax.all_gather(normed, 'tp', axis=1, tiled=True)  55.9 us
    all_gather x1, waiting for transfers between devices, layer(): mlp_full = lax.all_gather(normed_mlp, 'tp', axis=1, tiled=True)  51.6 us
    dot_general x1, matrix products, layer(): jnp.einsum('rcn,nd->rcd', attended, w_o, preferred_element_type=jnp.float32)  32.3 us
    dot_general x1, matrix products, attend(): jnp.einsum('rckgd,rskd->rkgcs', query_groups, k_cache, preferred_element_...  26.6 us
    reduce_sum x1, other arithmetic, attend(): attn_probs = jax.nn.softmax(scores, axis=-1).astype(jnp.bfloat16)  21.8 us
    dot_general x1, matrix products, mlp_partial(): jnp.einsum('rcf,fd->rcd', hidden_act, w_down, preferred_element_type=jnp....  19.3 us
  transfers between devices with their start and end apart: 4, of which 4 were waited for; matrix products, arithmetic and copies ran while one was open for 0% of the time, Pallas kernels for 0%

commit v1 on v0

v1 whole, which is shorter than its diff:
```python
import functools
import math

import jax
import jax.numpy as jnp
from jax import lax
from jax.experimental import pallas as pl
from jax.experimental.pallas import tpu as pltpu
from jax.sharding import PartitionSpec as P

ROPE_THETA = 1.0e6
NORM_EPS = 1.0e-6


def rms_norm(hidden, gain):
    wide_vals = hidden.astype(jnp.float32)
    inv_rms = lax.rsqrt(jnp.mean(wide_vals * wide_vals, axis=-1, keepdims=True) + NORM_EPS)
    return (wide_vals * inv_rms * gain.astype(jnp.float32)).astype(jnp.bfloat16)


def rotate_heads(heads, positions):
    half = heads.shape[-1] // 2
    inv_freq = ROPE_THETA ** (-(jnp.arange(half, dtype=jnp.float32) * 2.0) / heads.shape[-1])
    angles = positions.astype(jnp.float32)[..., None] * inv_freq
    cos_t = jnp.cos(angles)[..., None, :]
    sin_t = jnp.sin(angles)[..., None, :]
    wide = heads.astype(jnp.float32)
    first_half = wide[..., :half]
    second_half = wide[..., half:]
    rotated = jnp.concatenate([first_half * cos_t - second_half * sin_t, second_half * cos_t + first_half * sin_t], axis=-1)
    return rotated.astype(jnp.bfloat16)


def project(hidden, weight, bias):
    total = jnp.einsum("rcd,dn->rcn", hidden, weight, preferred_element_type=jnp.float32)
    return (total + bias.astype(jnp.float32)).astype(jnp.bfloat16)


NEG = -1.0e30

def attn_kernel(bq, sub, bk, p_ref, c_ref, q_ref, kn_ref, vn_ref, kc_ref, vc_ref, o_ref, ko_ref, vo_ref, shift, vext, m_s, acc_s):
    r = pl.program_id(0)
    qb = pl.program_id(1)
    slots, d = kc_ref.shape
    n_tok = kn_ref.shape[0]
    win = n_tok + 16
    prefix = p_ref[r]
    valid = c_ref[r]

    @pl.when(qb == 0)
    def _merge():
        start = pl.multiple_of(jnp.minimum((prefix // 16) * 16, slots - win), 16)
        off = prefix - start
        rows = lax.broadcasted_iota(jnp.int32, (win, d), 0) - off
        fresh = (rows >= 0) & (rows < valid)
        for new_ref, old_ref, out_ref in ((kn_ref, kc_ref, ko_ref), (vn_ref, vc_ref, vo_ref)):
            out_ref[...] = old_ref[...]
            shift[pl.ds(16, n_tok), :] = new_ref[...].astype(jnp.float32)
            moved = shift[pl.ds(16 - off, win), :]
            old = old_ref[pl.ds(start, win), :].astype(jnp.float32)
            out_ref[pl.ds(start, win), :] = jnp.where(fresh, moved, old).astype(out_ref.dtype)
        vext[:, :d] = vo_ref[...]
        vext[:, d:] = jnp.ones((slots, d), vext.dtype)

    scale2 = (d ** -0.5) * math.log2(math.e)
    m_s[...] = jnp.full_like(m_s, NEG)
    acc_s[...] = jnp.zeros_like(acc_s)
    row0 = qb * bq
    n_full = (prefix + jnp.minimum(row0, valid - 1) + 1) // bk
    n_all = pl.cdiv(prefix + jnp.minimum(row0 + bq - 1, valid - 1) + 1, bk)

    def step(j, masked):
        base = pl.multiple_of(j * bk, bk)
        keys = ko_ref[pl.ds(base, bk), :]
        vals = vext[pl.ds(base, bk), :]
        for t in range(bq // sub):
            sl = pl.ds(t * sub, sub)
            s = lax.dot_general(q_ref[sl, :], keys, (((1,), (1,)), ((), ())), preferred_element_type=jnp.float32)
            if masked:
                rid = lax.broadcasted_iota(jnp.int32, (sub, 1), 0) + (row0 + t * sub)
                lim = prefix + jnp.minimum(rid, valid - 1) - base
                s = jnp.where(lax.broadcasted_iota(jnp.int32, (sub, bk), 1) <= lim, s, NEG)
            m_prev = m_s[sl, :]
            m_new = jnp.maximum(m_prev, jnp.max(s, axis=1, keepdims=True))
            m_s[sl, :] = m_new
            a = jnp.exp2((m_prev - m_new) * scale2)
            p = jnp.exp2((s - m_new[:, :1]) * scale2).astype(vext.dtype)
            pv = lax.dot_general(p, vals, (((1,), (0,)), ((), ())), preferred_element_type=jnp.float32)
            acc_s[sl, :] = acc_s[sl, :] * jnp.concatenate([a, a], axis=1) + pv

    def full_body(j, _):
        step(j, False)
        return 0

    def edge_body(j, _):
        step(j, True)
        return 0

    lax.fori_loop(0, n_full, full_body, 0)
    lax.fori_loop(n_full, n_all, edge_body, 0)
    o_ref[...] = (acc_s[:, :d] / acc_s[:, d:]).astype(o_ref.dtype)


def attention(q, kn, vn, kc, vc, prefix, valid, bq=1024, sub=128, bk=2048):
    n_req, n_tok, d = q.shape
    slots = kc.shape[1]
    sq = pl.Squeezed()
    tok = pl.BlockSpec((sq, bq, d), lambda r, b, *_: (r, b, 0))
    new = pl.BlockSpec((sq, n_tok, d), lambda r, b, *_: (r, 0, 0))
    cache = pl.BlockSpec((sq, slots, d), lambda r, b, *_: (r, 0, 0))
    return pl.pallas_call(
        functools.partial(attn_kernel, bq, sub, bk),
        grid_spec=pltpu.PrefetchScalarGridSpec(
            num_scalar_prefetch=2,
            grid=(n_req, n_tok // bq),
            in_specs=[tok, new, new, cache, cache],
            out_specs=[tok, cache, cache],
            scratch_shapes=[
                pltpu.VMEM((n_tok + 32, d), jnp.float32),
                pltpu.VMEM((slots, 2 * d), jnp.bfloat16),
                pltpu.VMEM((bq, d), jnp.float32),
                pltpu.VMEM((bq, 2 * d), jnp.float32),
            ],
        ),
        out_shape=[
            jax.ShapeDtypeStruct(q.shape, q.dtype),
            jax.ShapeDtypeStruct(kc.shape, kc.dtype),
            jax.ShapeDtypeStruct(vc.shape, vc.dtype),
        ],
        cost_estimate=pl.CostEstimate(flops=8 * n_req * n_tok * slots * d, bytes_accessed=8 * n_req * slots * d, transcendentals=n_req * n_tok * slots),
        compiler_params=pltpu.CompilerParams(vmem_limit_bytes=56 * 2**20, dimension_semantics=("arbitrary", "arbitrary")),
        name="attend",
    )(prefix, valid, q, kn, vn, kc, vc)


MESH = pl.DeviceIdType.MESH


def remote(src, dst, send, recv, target):
    return pltpu.make_async_remote_copy(src_ref=src, dst_ref=dst, send_sem=send, recv_sem=recv, device_id={"tp": target}, device_id_type=MESH)


def tail_kernel(n_tp, o_hbm, x_ref, g_ref, wo_hbm, wg_hbm, wu_hbm, wd_hbm, out_ref,
                o_v, o_all, wo, wg, wu, wd, x1, rows, sums_in, sums_out, part_in, part_out, kept,
                load_sem, own_sem, o_send, o_recv, ring_send, ring_recv, pair_send, pair_recv, sum_send, sum_recv, part_send, part_recv):
    nz = n_tp // 2
    me = lax.axis_index("tp")
    core = lax.rem(me, 2)
    chip = me // 2
    up = lax.rem(chip + 1, nz) * 2 + core
    down = lax.rem(chip + nz - 1, nz) * 2 + core
    pair = chip * 2 + 1 - core
    towards = (up, down)
    n_req, n_rows, width = x_ref.shape
    d = o_v.shape[-1]

    loads = [pltpu.make_async_copy(s, t, load_sem.at[i]) for i, (s, t) in enumerate(((o_hbm, o_v), (wo_hbm, wo), (wg_hbm, wg), (wu_hbm, wu), (wd_hbm, wd)))]
    for c in loads:
        c.start()

    barrier = pltpu.get_barrier_semaphore()
    for k in range(1, n_tp):
        pl.semaphore_signal(barrier, inc=1, device_id={"tp": lax.rem(me + k, n_tp)}, device_id_type=MESH)
    pl.semaphore_wait(barrier, n_tp - 1)

    loads[0].wait()
    mine = pl.ds(pl.multiple_of(me * d, d), d)
    sends = []
    for k in range(1, n_tp):
        there = lax.rem(me + k, n_tp)
        c = remote(o_v.at[:, pl.ds(pl.multiple_of(there * n_rows, n_rows), n_rows), :], o_all.at[:, :, mine], o_send.at[k], o_recv.at[k], there)
        c.start()
        sends.append(c)
    o_all[:, :, mine] = o_v[:, pl.ds(pl.multiple_of(me * n_rows, n_rows), n_rows), :]
    loads[1].wait()
    for c in sends:
        c.wait_recv()

    mixed = jnp.dot(o_all[...].reshape(n_req * n_rows, width), wo[...], preferred_element_type=jnp.float32).astype(jnp.bfloat16)
    resid = (x_ref[...].reshape(n_req * n_rows, width).astype(jnp.float32) + mixed.astype(jnp.float32)).astype(jnp.bfloat16)
    x1[...] = resid.reshape(x1.shape)
    wide = resid.astype(jnp.float32)
    inv = lax.rsqrt(jnp.mean(wide * wide, axis=-1, keepdims=True) + NORM_EPS)
    normed = (wide * inv * g_ref[...].astype(jnp.float32)).astype(jnp.bfloat16)
    rows[0, :, 0] = normed.reshape(n_req, n_rows, width)

    for i in (2, 3, 4):
        loads[i].wait()

    def ring_copy(s, way):
        return remote(rows.at[s, way, 0], rows.at[s + 1, way, 0], ring_send.at[s, way], ring_recv.at[s + 1, way], towards[way])

    def pair_copy(s, way):
        return remote(rows.at[s, way, 0], rows.at[s, way, 1], pair_send.at[s, way], pair_recv.at[s, way], pair)

    def part_copy(s):
        return remote(part_out.at[s], part_in.at[s], part_send.at[s], part_recv.at[s], pair)

    def sum_copy(s, way):
        return remote(sums_out.at[s, way], sums_in.at[s + 1, way], sum_send.at[s, way], sum_recv.at[s + 1, way], towards[way])

    def step(s, _):
        for way in range(2):
            @pl.when(s > 0)
            def _():
                ring_copy(s - 1, way).wait_recv()

            @pl.when(s < nz - 1)
            def _():
                ring_copy(s, way).start()

            pair_copy(s, way).start()
        for way in range(2):
            pair_copy(s, way).wait_recv()
        lhs = rows[s].reshape(4 * n_rows, width)
        gate = jnp.dot(lhs, wg[...], preferred_element_type=jnp.float32)
        lift = jnp.dot(lhs, wu[...], preferred_element_type=jnp.float32)
        act = (jax.nn.silu(gate) * lift).astype(jnp.bfloat16)
        part = jnp.dot(act, wd[...], preferred_element_type=jnp.float32).reshape(2, 2, n_rows, width)
        part_out[s] = part[:, 1].astype(jnp.bfloat16)
        part_copy(s).start()
        kept[jnp.minimum(s, 1)] = part[:, 0]

        @pl.when(s > 0)
        def _():
            part_copy(s).wait_recv()
            for way in range(2):
                @pl.when(s > 1)
                def _():
                    sum_copy(s - 1, way).wait_recv()
                    sums_out[s, way] = (kept[1, way] + part_in[s, way].astype(jnp.float32) + sums_in[s, way].astype(jnp.float32)).astype(jnp.bfloat16)

                @pl.when(s == 1)
                def _():
                    sums_out[s, way] = (kept[1, way] + part_in[s, way].astype(jnp.float32)).astype(jnp.bfloat16)

                sum_copy(s, way).start()
        return 0

    lax.fori_loop(0, nz, step, 0)

    part_copy(0).wait_recv()
    for way in range(2):
        sum_copy(nz - 1, way).wait_recv()
        total = kept[0, way] + part_in[0, way].astype(jnp.float32) + sums_in[nz, way].astype(jnp.float32)
        out_ref[way] = (x1[way].astype(jnp.float32) + total.astype(jnp.bfloat16).astype(jnp.float32)).astype(jnp.bfloat16)

    for c in sends:
        c.wait_send()
    for s in range(nz):
        part_copy(s).wait_send()
        for way in range(2):
            pair_copy(s, way).wait_send()
            if s < nz - 1:
                ring_copy(s, way).wait_send()
            if s > 0:
                sum_copy(s, way).wait_send()


def tail(n_tp, o, x, gain, w_o, w_gate, w_up, w_down):
    n_req, n_rows, width = x.shape
    ffn = w_gate.shape[1]
    nz = n_tp // 2
    bf = jnp.bfloat16
    any_spec = pl.BlockSpec(memory_space=pl.ANY)
    vm = pl.BlockSpec(memory_space=pltpu.VMEM)
    dma = pltpu.SemaphoreType.DMA
    return pl.pallas_call(
        functools.partial(tail_kernel, n_tp),
        out_shape=jax.ShapeDtypeStruct(x.shape, x.dtype),
        in_specs=[any_spec, vm, vm, any_spec, any_spec, any_spec, any_spec],
        out_specs=vm,
        scratch_shapes=[
            pltpu.VMEM(o.shape, bf),
            pltpu.VMEM((n_req, n_rows, width), bf),
            pltpu.VMEM(w_o.shape, bf),
            pltpu.VMEM(w_gate.shape, bf),
            pltpu.VMEM(w_up.shape, bf),
            pltpu.VMEM(w_down.shape, bf),
            pltpu.VMEM((n_req, n_rows, width), bf),
            pltpu.VMEM((nz, 2, 2, n_rows, width), bf),
            pltpu.VMEM((nz + 1, 2, n_rows, width), bf),
            pltpu.VMEM((nz, 2, n_rows, width), bf),
            pltpu.VMEM((nz, 2, n_rows, width), bf),
            pltpu.VMEM((nz, 2, n_rows, width), bf),
            pltpu.VMEM((2, 2, n_rows, width), jnp.float32),
            dma((5,)), dma, dma((n_tp,)), dma((n_tp,)),
            dma((nz, 2)), dma((nz, 2)), dma((nz, 2)), dma((nz, 2)),
            dma((nz, 2)), dma((nz + 1, 2)), dma((nz,)), dma((nz,)),
        ],
        compiler_params=pltpu.CompilerParams(vmem_limit_bytes=62 * 2**20, collective_id=1, has_side_effects=True),
        cost_estimate=pl.CostEstimate(flops=6 * n_tp * n_req * n_rows * width * ffn, bytes_accessed=20 * 2**20, transcendentals=0),
        name="tail",
    )(o, x, gain.reshape(1, width), w_o, w_gate, w_up, w_down)


def solution(mesh):
    n_tp = mesh.shape["tp"]
    row_spec = P("dp", "tp", None)
    cache_spec = P("dp", None, "tp", None)
    req_spec = P("dp")
    rep_spec = P(None)
    col_spec = P(None, "tp")
    bias_spec = P("tp")
    down_spec = P("tp", None)

    def layer(x_rows, k_cache, v_cache, prefix, valid, g_attn, w_q, b_q, w_k, b_k, w_v, b_v, w_o, g_mlp, w_gate, w_up, w_down):
        normed = rms_norm(x_rows, g_attn)
        normed_full = lax.all_gather(normed, "tp", axis=1, tiled=True)
        n_req, n_tokens = normed_full.shape[0], normed_full.shape[1]
        head_dim = k_cache.shape[-1]
        positions = prefix[:, None] + jnp.arange(n_tokens, dtype=jnp.int32)[None, :]
        q = rotate_heads(project(normed_full, w_q, b_q).reshape(n_req, n_tokens, -1, head_dim), positions)
        k = rotate_heads(project(normed_full, w_k, b_k).reshape(n_req, n_tokens, -1, head_dim), positions)
        v = project(normed_full, w_v, b_v)
        w_o, q = lax.optimization_barrier((w_o, q))
        w_o_full = lax.all_gather(w_o, "tp", axis=0, tiled=True)
        flat = (n_req, -1, head_dim)
        o, k_out, v_out = attention(q.reshape(flat), k.reshape(flat), v, k_cache.reshape(flat), v_cache.reshape(flat), prefix, valid)
        out = tail(n_tp, o, x_rows, g_mlp, w_o_full, w_gate, w_up, w_down)
        return out, k_out.reshape(k_cache.shape), v_out.reshape(v_cache.shape)

    in_specs = (row_spec, cache_spec, cache_spec, req_spec, req_spec, rep_spec, col_spec, bias_spec, col_spec, bias_spec, col_spec, bias_spec, down_spec, rep_spec, col_spec, col_spec, down_spec)
    return jax.shard_map(layer, mesh=mesh, in_specs=in_specs, out_specs=(row_spec, cache_spec, cache_spec), check_vma=False)
```

time: 432 us -> 253 us (0.59)
  waiting for transfers between devices: 239 us -> 57.4 us
  Pallas kernels: 0 us -> 139 us
  matrix products: 106 us -> 16.1 us
  other arithmetic: 40.2 us -> 15.2 us
  local copies, waits for them, and re-layouts: 23.7 us -> 9.92 us
  loops' own time: 7.57 us -> 0 us
    pallas_call x0 -> x2, Pallas kernels: none -> 139 us  [the longest x1 108 us: tail(): pl.pallas_call(functools.partial(tail_kernel, n_tp), out_shape=jax.ShapeD...]
    reduce_scatter x2 -> x0, waiting for transfers between devices: 132 us -> none  [the longest x1 66.3 us: layer(): lax.psum_scatter(down_part, 'tp', scatter_dimension=1, tiled=True)]
    dot_general x4 -> x0, matrix products: 89.1 us -> none  [the longest x1 32.3 us: layer(): jnp.einsum('rcn,nd->rcd', attended, w_o, preferred_element_type=jnp.float32)]
    all_gather x1, waiting for transfers between devices: 51.6 us -> 3.23 us  [layer(): w_o_full = lax.all_gather(w_o, 'tp', axis=0, tiled=True)]
    reduce_sum x1 -> x0, other arithmetic: 21.8 us -> none  [attend(): attn_probs = jax.nn.softmax(scores, axis=-1).astype(jnp.bfloat16)]
    dynamic_update_slice x4 -> x0, local copies, waits for them, and re-layouts: 9.11 us -> none  [body(): return lax.dynamic_update_slice(buffer, merged, (req_idx, start, 0, 0))]
    another operation x2 -> x0, loops' own time: 7.57 us -> none  [write_rows(): return lax.fori_loop(0, cache.shape[0], body, cache)]
    dynamic_slice x12 -> x0, local copies, waits for them, and re-layouts: 7.26 us -> none  [the longest x4 2.5 us: body(): merged = jnp.where(row_ids < valid[req_idx], fresh, old_rows)]
  transfers between devices with their start and end apart: 4 -> 2, of which waited for: 4 -> 2; matrix products, arithmetic and copies ran while one was open for 0% -> 8% of each run, Pallas kernels for 0% -> 12%
where the time goes in v1:
time: 253 us; the launch traced here: 252 us
  Pallas kernels  139 us (55%)
  waiting for transfers between devices  57.4 us (23%)
  matrix products  16.1 us (6%)
  other arithmetic  15.2 us (6%)
  between operations  14.1 us (6%)
  local copies, waits for them, and re-layouts  9.92 us (4%)
    pallas_call x1, Pallas kernels, tail(): pl.pallas_call(functools.partial(tail_kernel, n_tp), out_shape=jax.ShapeD...  108 us
    all_gather x1, waiting for transfers between devices, layer(): normed_full = lax.all_gather(normed, 'tp', axis=1, tiled=True)  54.1 us
    pallas_call x1, Pallas kernels, attention(): pl.pallas_call(functools.partial(attn_kernel, bq, sub, bk), grid_spec=plt...  31.1 us
    dot_general x3, matrix products, project(): jnp.einsum('rcd,dn->rcn', hidden, weight, preferred_element_type=jnp.floa...  16.1 us
    unnamed x13, local copies, waits for them, and re-layouts  9.32 us
    concatenate x3, other arithmetic, rotate_heads(): jnp.concatenate([first_half * cos_t - second_half * sin_t, second_half *...  9.11 us
  transfers between devices with their start and end apart: 2, of which 2 were waited for; matrix products, arithmetic and copies ran while one was open for 8% of the time, Pallas kernels for 12%

profile of v1, /device:TPU:28, one launch (start us, length us, event | category | flops | bytes accessed | tf_op | source)
XLA Modules:
  0.0 252.2 jit_solution(11303616846899639641)
XLA Ops:
  7.2 0.1 all-gather.3.cloned.1.call-start
  7.3 0.7 convert_element_type.61
  8.0 1.2 fusion.15
  9.2 2.0 fusion.17
  11.3 0.1 all-gather.3.cloned.1.call-update
  11.3 0.1 all-gather.5.cloned.1.call-start
  11.4 0.7 convert_element_type.68
  12.1 0.7 convert_element_type.63
  12.7 0.7 add_convert_fusion
  13.5 54.1 %all-gather.3.cloned.1.call-done = bf16[2,1024,2048]{2,1,0:T(8,128)(2,1)} async-done(((bf16[2,64,2048]{2,1,0:T(8,128)(2,1)}), bf16[2,1024,2048]{2,1,0:T(8,128)(2,1)}) %all-gather.3.cloned.1.call-update) | async-done | bytes 8388624 | tf_op jit(solution)/shard_map/all_gather | solution.py:309
  67.5 5.9 %fusion.12 = f32[2,1024,1,128]{3,1,0,2:T(8,128)S(1)} fusion(bf16[2,1024,2048]{2,1,0:T(8,128)(2,1)} %all-gather.3.cloned.1.call-done, bf16[2048,128]{1,0:T(8,128)(2,1)S(1)} %copy-done, f32[128]{0:T(128)S(1)} %convert_element_type.68), kind=kOutput, calls=%fused_computation.19 | convolution fusion | flops 1074528256 | bytes 9961984 | tf_op jit(solution)/shard_map/rcd,dn->rcn/dot_general | solution.py:35
  73.5 3.5 %fusion.14 = f32[2,1024,1,128]{3,1,0,2:T(8,128)S(1)} fusion(bf16[2,1024,2048]{2,1,0:T(8,128)(2,1)S(1)} %copy-done.3, bf16[2048,128]{1,0:T(8,128)(2,1)} %param.23, f32[128]{0:T(128)S(1)} %convert_element_type.63), kind=kOutput, calls=%fused_computation.21 | convolution fusion | flops 1074528256 | bytes 9961984 | tf_op jit(solution)/shard_map/rcd,dn->rcn/dot_general | solution.py:35
  77.0 5.7 %fusion.30 = (bf16[2,1024,64]{2,1,0:T(8,128)(2,1)}, bf16[2,1024,64]{2,1,0:T(8,128)(2,1)}, bf16[2,1024,1,64]{3,1,0,2:T(8,128)(2,1)S(1)}, bf16[2,1024,1,64]{3,1,0,2:T(8,128)(2,1)S(1)}) fusion(f32[2,1024,1,128]{3,1,0,2:T(8,128)S(1)} %fusion.12, f32[64]{0:T(128)S(1)} %multiply_power_fusion, f32[2,1024]{1,0:T(2,128)S(1)} %add_convert_fusion, ...), kind=kLoop, calls=%fused_computation.39 | loop fusion | flops 2228224 | bytes 3154176 | tf_op jit(solution)/shard_map/concatenate | solution.py:30
  82.8 1.1 pad_maximum_fusion
  83.9 0.1 all-gather.5.cloned.1.call-update
  84.0 2.8 %copy.24.wg_hbm = bf16[2048,688]{1,0:T(8,128)(2,1)} copy(bf16[2048,688]{0,1:T(8,128)(2,1)S(1)} %copy-done.1) | data formatting | bytes 5636096 | tf_op args[14]
  86.8 4.6 %copy.25.wu_hbm = bf16[2048,688]{1,0:T(8,128)(2,1)} copy(bf16[2048,688]{0,1:T(8,128)(2,1)} %param.32) | data formatting | bytes 5636096 | tf_op args[15]
  91.4 0.6 reshape.125.g_ref
  92.0 2.3 pad_maximum_fusion.1.kn_ref
  94.3 6.6 %fusion.10.vn_ref = bf16[2,1024,128]{2,1,0:T(8,128)(2,1)} fusion(bf16[2,1024,2048]{2,1,0:T(8,128)(2,1)} %all-gather.3.cloned.1.call-done, bf16[2048,128]{1,0:T(8,128)(2,1)} %param.27, f32[128]{0:T(128)S(1)} %convert_element_type.72), kind=kOutput, calls=%fused_computation.17 | convolution fusion | flops 1074266112 | bytes 9437696 | tf_op jit(solution)/shard_map/rcd,dn->rcn/dot_general | solution.py:35
  100.8 31.1 %attend.1 = (bf16[2,1024,128]{2,1,0:T(8,128)(2,1)}, bf16[2,8192,128]{2,1,0:T(8,128)(2,1)}, bf16[2,8192,128]{2,1,0:T(8,128)(2,1)}) custom-call(s32[2]{0:T(128)} %p_ref.1, s32[2]{0:T(128)} %c_ref.1, bf16[2,1024,128]{2,1,0:T(8,128)(2,1)} %bitcast.35, bf16[2,1024,128]{2,1,0:T(8,128)(2,1)} %pad_maximum_fusion.1.kn_ref, bf16[2,1024,128]{2,1,0:T(8,128)(2,1)} %fusion.10.vn_ref, ...), custom_call_target="tpu_custom_call" | custom-call | flops 17179869184 | bytes 16777216 | tf_op jit(solution)/shard_map/attend/pallas_call | solution.py:111
  131.9 3.2 %all-gather.5.cloned.1.call-done.wo_hbm = bf16[2048,2048]{1,0:T(8,128)(2,1)} async-done(((bf16[128,2048]{1,0:T(8,128)(2,1)}), bf16[2048,2048]{1,0:T(8,128)(2,1)}) %all-gather.5.cloned.1.call-update) | async-done | bytes 8388624 | tf_op jit(solution)/shard_map/all_gather | solution.py:317
  135.1 108.3 %tail.1 = bf16[2,64,2048]{2,1,0:T(8,128)(2,1)} custom-call(bf16[2,1024,128]{2,1,0:T(8,128)(2,1)} %get-tuple-element.9.o_hbm, bf16[2,64,2048]{2,1,0:T(8,128)(2,1)} %x_ref.1, bf16[1,2048]{1,0:T(2,128)(2,1)} %reshape.125.g_ref, bf16[2048,2048]{1,0:T(8,128)(2,1)} %all-gather.5.cloned.1.call-done.wo_hbm, bf16[2048,688]{1,0:T(8,128)(2,1)} %copy.24.wg_hbm, ...), custom_call_target="tpu_custom_call" | custom-call | flops 17314086912 | bytes 20971520 | tf_op jit(solution)/shard_map/tail/pallas_call | solution.py:268
  243.5 1.9 copy.35
  (13 shorter events, 0.1 us)
Async XLA Ops:
  7.2 60.3 %copy-start = (bf16[2048,128]{1,0:T(8,128)(2,1)S(1)}, bf16[2048,128]{1,0:T(8,128)(2,1)}, u32[]{:S(2)}) copy-start(bf16[2048,128]{1,0:T(8,128)(2,1)} %param.25) | copy-start | bytes 1572868
  7.2 60.3 %all-gather.3.cloned.1.call-start = ((), (), s32[]{:S(2)}) async-start(), calls=%async_computation | async-start | bytes 8912896 | tf_op jit(solution)/shard_map/all_gather | solution.py:309
  11.3 123.8 %all-gather.5.cloned.1.call-start = ((), (), s32[]{:S(2)}) async-start(), calls=%async_computation.1 | async-start | bytes 8912896 | tf_op jit(solution)/shard_map/all_gather | solution.py:317
  67.5 5.9 %copy-start.3 = (bf16[2,1024,2048]{2,1,0:T(8,128)(2,1)S(1)}, bf16[2,1024,2048]{2,1,0:T(8,128)(2,1)}, u32[]{:S(2)}) copy-start(bf16[2,1024,2048]{2,1,0:T(8,128)(2,1)} %all-gather.3.cloned.1.call-done) | copy-start | bytes 25165828
  73.5 10.5 %copy-start.4 = (bf16[128]{0:T(256)(128)(2,1)S(1)}, bf16[128]{0:T(256)(128)(2,1)}, u32[]{:S(2)}) copy-start(bf16[128]{0:T(256)(128)(2,1)} %param.28) | copy-start | bytes 772
  73.5 10.5 %copy-start.1 = (bf16[2048,688]{0,1:T(8,128)(2,1)S(1)}, bf16[2048,688]{0,1:T(8,128)(2,1)}, u32[]{:S(2)}) copy-start(bf16[2048,688]{0,1:T(8,128)(2,1)} %param.31) | copy-start | bytes 8454148
  82.8 8.6 %copy-start.2 = (bf16[2048]{0:T(1024)(128)(2,1)S(1)}, bf16[2048]{0:T(1024)(128)(2,1)}, u32[]{:S(2)}) copy-start(bf16[2048]{0:T(1024)(128)(2,1)} %param.30) | copy-start | bytes 12292
Sparse Core Ops, SparseCore 0:
  11.4 56.0 all-gather.2
  84.1 51.0 all-gather.4

commit v2 on v1

--- a/solution.py
+++ b/solution.py
@@ -10,30 +10,6 @@
 
 ROPE_THETA = 1.0e6
 NORM_EPS = 1.0e-6
-
-
-def rms_norm(hidden, gain):
-    wide_vals = hidden.astype(jnp.float32)
-    inv_rms = lax.rsqrt(jnp.mean(wide_vals * wide_vals, axis=-1, keepdims=True) + NORM_EPS)
-    return (wide_vals * inv_rms * gain.astype(jnp.float32)).astype(jnp.bfloat16)
-
-
-def rotate_heads(heads, positions):
-    half = heads.shape[-1] // 2
-    inv_freq = ROPE_THETA ** (-(jnp.arange(half, dtype=jnp.float32) * 2.0) / heads.shape[-1])
-    angles = positions.astype(jnp.float32)[..., None] * inv_freq
-    cos_t = jnp.cos(angles)[..., None, :]
-    sin_t = jnp.sin(angles)[..., None, :]
-    wide = heads.astype(jnp.float32)
-    first_half = wide[..., :half]
-    second_half = wide[..., half:]
-    rotated = jnp.concatenate([first_half * cos_t - second_half * sin_t, second_half * cos_t + first_half * sin_t], axis=-1)
-    return rotated.astype(jnp.bfloat16)
-
-
-def project(hidden, weight, bias):
-    total = jnp.einsum("rcd,dn->rcn", hidden, weight, preferred_element_type=jnp.float32)
-    return (total + bias.astype(jnp.float32)).astype(jnp.bfloat16)
 
 
 NEG = -1.0e30
@@ -142,7 +118,7 @@
 
 def tail_kernel(n_tp, o_hbm, x_ref, g_ref, wo_hbm, wg_hbm, wu_hbm, wd_hbm, out_ref,
                 o_v, o_all, wo, wg, wu, wd, x1, rows, sums_in, sums_out, part_in, part_out, kept,
-                load_sem, own_sem, o_send, o_recv, ring_send, ring_recv, pair_send, pair_recv, sum_send, sum_recv, part_send, part_recv):
+                load_sem, o_send, o_recv, ring_send, ring_recv, pair_send, pair_recv, sum_send, sum_recv, part_send, part_recv):
     nz = n_tp // 2
     me = lax.axis_index("tp")
     core = lax.rem(me, 2)
@@ -213,8 +189,8 @@
         for way in range(2):
             pair_copy(s, way).wait_recv()
         lhs = rows[s].reshape(4 * n_rows, width)
-        gate = jnp.dot(lhs, wg[...], preferred_element_type=jnp.float32)
-        lift = jnp.dot(lhs, wu[...], preferred_element_type=jnp.float32)
+        gate = lax.dot_general(lhs, wg[...], (((1,), (1,)), ((), ())), preferred_element_type=jnp.float32)
+        lift = lax.dot_general(lhs, wu[...], (((1,), (1,)), ((), ())), preferred_element_type=jnp.float32)
         act = (jax.nn.silu(gate) * lift).astype(jnp.bfloat16)
         part = jnp.dot(act, wd[...], preferred_element_type=jnp.float32).reshape(2, 2, n_rows, width)
         part_out[s] = part[:, 1].astype(jnp.bfloat16)
@@ -259,7 +235,7 @@
 
 def tail(n_tp, o, x, gain, w_o, w_gate, w_up, w_down):
     n_req, n_rows, width = x.shape
-    ffn = w_gate.shape[1]
+    ffn = w_gate.shape[0]
     nz = n_tp // 2
     bf = jnp.bfloat16
     any_spec = pl.BlockSpec(memory_space=pl.ANY)
@@ -284,7 +260,7 @@
             pltpu.VMEM((nz, 2, n_rows, width), bf),
             pltpu.VMEM((nz, 2, n_rows, width), bf),
             pltpu.VMEM((2, 2, n_rows, width), jnp.float32),
-            dma((5,)), dma, dma((n_tp,)), dma((n_tp,)),
+            dma((5,)), dma((n_tp,)), dma((n_tp,)),
             dma((nz, 2)), dma((nz, 2)), dma((nz, 2)), dma((nz, 2)),
             dma((nz, 2)), dma((nz + 1, 2)), dma((nz,)), dma((nz,)),
         ],
@@ -292,6 +268,110 @@
         cost_estimate=pl.CostEstimate(flops=6 * n_tp * n_req * n_rows * width * ffn, bytes_accessed=20 * 2**20, transcendentals=0),
         name="tail",
     )(o, x, gain.reshape(1, width), w_o, w_gate, w_up, w_down)
+
+
+def front_kernel(n_tp, p_ref, x_ref, g_ref, f_ref, b_ref, wq_hbm, wk_hbm, wv_hbm, q_ref, k_ref, v_ref, w, rows, load_sem, ring_send, ring_recv, pair_send, pair_recv):
+    nz = n_tp // 2
+    me = lax.axis_index("tp")
+    core = lax.rem(me, 2)
+    chip = me // 2
+    up = lax.rem(chip + 1, nz) * 2 + core
+    down = lax.rem(chip + nz - 1, nz) * 2 + core
+    pair = chip * 2 + 1 - core
+    towards = (up, down)
+    n_req, n_rows, width = x_ref.shape
+    d = q_ref.shape[-1]
+
+    loads = [pltpu.make_async_copy(s, w.at[:, pl.ds(i * d, d)], load_sem.at[i]) for i, s in enumerate((wq_hbm, wk_hbm, wv_hbm))]
+    for c in loads:
+        c.start()
+
+    barrier = pltpu.get_barrier_semaphore()
+    for there in (up, down, pair):
+        pl.semaphore_signal(barrier, inc=1, device_id={"tp": there}, device_id_type=MESH)
+
+    wide = x_ref[...].astype(jnp.float32)
+    inv = lax.rsqrt(jnp.mean(wide * wide, axis=-1, keepdims=True) + NORM_EPS)
+    rows[0, :, 0] = (wide * inv * g_ref[...].astype(jnp.float32)).astype(jnp.bfloat16)
+    pl.semaphore_wait(barrier, 3)
+
+    def ring_copy(s, way):
+        return remote(rows.at[s, way, 0], rows.at[s + 1, way, 0], ring_send.at[s, way], ring_recv.at[s + 1, way], towards[way])
+
+    def pair_copy(s, way):
+        return remote(rows.at[s, way, 0], rows.at[s, way, 1], pair_send.at[s, way], pair_recv.at[s, way], pair)
+
+    def step(s, _):
+        for way in range(2):
+            @pl.when(s > 0)
+            def _():
+                ring_copy(s - 1, way).wait_recv()
+
+            @pl.when(s < nz - 1)
+            def _():
+                ring_copy(s, way).start()
+
+            pair_copy(s, way).start()
+
+        @pl.when(s == 0)
+        def _():
+            for c in loads:
+                c.wait()
+
+        for way in range(2):
+            pair_copy(s, way).wait_recv()
+        lhs = rows[s].reshape(4 * n_rows, width)
+        total = jnp.dot(lhs, w[...], preferred_element_type=jnp.float32)
+        got = (total + b_ref[...].astype(jnp.float32)).astype(jnp.bfloat16)
+        sign = jnp.where(lax.broadcasted_iota(jnp.int32, (n_rows, d), 1) < d // 2, -1.0, 1.0)
+        for way in range(2):
+            home = lax.rem(chip + (nz - s if way == 0 else s), nz)
+            for other in range(2):
+                off = pl.multiple_of((home * 2 + (core if other == 0 else 1 - core)) * n_rows, n_rows)
+                at = pl.ds(off, n_rows)
+                spot = (lax.broadcasted_iota(jnp.int32, (n_rows, d), 0) + (p_ref[way] + off)).astype(jnp.float32)
+                angle = spot * f_ref[...]
+                cos_t = jnp.cos(angle)
+                sin_t = jnp.sin(angle) * sign
+                mine = got[(way * 2 + other) * n_rows:(way * 2 + other + 1) * n_rows]
+                for ref, part in ((q_ref, mine[:, :d]), (k_ref, mine[:, d:2 * d])):
+                    part = part.astype(jnp.float32)
+                    ref[way, at, :] = (part * cos_t + pltpu.roll(part, d // 2, 1) * sin_t).astype(jnp.bfloat16)
+                v_ref[way, at, :] = mine[:, 2 * d:]
+        return 0
+
+    lax.fori_loop(0, nz, step, 0)
+    for s in range(nz):
+        for way in range(2):
+            pair_copy(s, way).wait_send()
+            if s < nz - 1:
+                ring_copy(s, way).wait_send()
+
+
+def front(n_tp, x, gain, prefix, freq, bias, w_q, w_k, w_v):
+    n_req, n_rows, width = x.shape
+    d = w_q.shape[1]
+    nz = n_tp // 2
+    n_tok = n_rows * n_tp
+    bf = jnp.bfloat16
+    any_spec = pl.BlockSpec(memory_space=pl.ANY)
+    vm = pl.BlockSpec(memory_space=pltpu.VMEM)
+    dma = pltpu.SemaphoreType.DMA
+    made = jax.ShapeDtypeStruct((n_req, n_tok, d), bf)
+    return pl.pallas_call(
+        functools.partial(front_kernel, n_tp),
+        out_shape=[made, made, made],
+        in_specs=[pl.BlockSpec(memory_space=pltpu.SMEM), vm, vm, vm, vm, any_spec, any_spec, any_spec],
+        out_specs=[vm, vm, vm],
+        scratch_shapes=[
+            pltpu.VMEM((width, 3 * d), bf),
+            pltpu.VMEM((nz, 2, 2, n_rows, width), bf),
+            dma((3,)), dma((nz, 2)), dma((nz, 2)), dma((nz, 2)), dma((nz, 2)),
+        ],
+        compiler_params=pltpu.CompilerParams(vmem_limit_bytes=40 * 2**20, collective_id=2, has_side_effects=True),
+        cost_estimate=pl.CostEstimate(flops=6 * n_req * n_tok * width * d, bytes_accessed=4 * 2**20, transcendentals=0),
+        name="front",
+    )(prefix, x, gain.reshape(1, width), freq, bias, w_q, w_k, w_v)
 
 
 def solution(mesh):
@@ -305,19 +385,17 @@
     down_spec = P("tp", None)
 
     def layer(x_rows, k_cache, v_cache, prefix, valid, g_attn, w_q, b_q, w_k, b_k, w_v, b_v, w_o, g_mlp, w_gate, w_up, w_down):
-        normed = rms_norm(x_rows, g_attn)
-        normed_full = lax.all_gather(normed, "tp", axis=1, tiled=True)
-        n_req, n_tokens = normed_full.shape[0], normed_full.shape[1]
-        head_dim = k_cache.shape[-1]
-        positions = prefix[:, None] + jnp.arange(n_tokens, dtype=jnp.int32)[None, :]
-        q = rotate_heads(project(normed_full, w_q, b_q).reshape(n_req, n_tokens, -1, head_dim), positions)
-        k = rotate_heads(project(normed_full, w_k, b_k).reshape(n_req, n_tokens, -1, head_dim), positions)
-        v = project(normed_full, w_v, b_v)
+        n_req, head_dim = x_rows.shape[0], k_cache.shape[-1]
+        half = jnp.arange(head_dim // 2, dtype=jnp.float32)
+        freq = ROPE_THETA ** (-(half * 2.0) / head_dim)
+        freq = jnp.concatenate([freq, freq])[None]
+        bias = jnp.concatenate([b_q, b_k, b_v])[None]
+        q, k, v = front(n_tp, x_rows, g_attn, prefix, freq, bias, w_q, w_k, w_v)
         w_o, q = lax.optimization_barrier((w_o, q))
         w_o_full = lax.all_gather(w_o, "tp", axis=0, tiled=True)
         flat = (n_req, -1, head_dim)
-        o, k_out, v_out = attention(q.reshape(flat), k.reshape(flat), v, k_cache.reshape(flat), v_cache.reshape(flat), prefix, valid)
-        out = tail(n_tp, o, x_rows, g_mlp, w_o_full, w_gate, w_up, w_down)
+        o, k_out, v_out = attention(q, k, v, k_cache.reshape(flat), v_cache.reshape(flat), prefix, valid)
+        out = tail(n_tp, o, x_rows, g_mlp, w_o_full, w_gate.T, w_up.T, w_down)
         return out, k_out.reshape(k_cache.shape), v_out.reshape(v_cache.shape)
 
     in_specs = (row_spec, cache_spec, cache_spec, req_spec, req_spec, rep_spec, col_spec, bias_spec, col_spec, bias_spec, col_spec, bias_spec, down_spec, rep_spec, col_spec, col_spec, down_spec)

time: 253 us -> 241 us (0.953)
  Pallas kernels: 139 us -> 193 us
  waiting for transfers between devices: 57.4 us -> 21.2 us
  matrix products: 16.1 us -> 0 us
  other arithmetic: 15.2 us -> 0.78 us
    all_gather x1 -> x0, waiting for transfers between devices: 54.1 us -> none  [layer(): normed_full = lax.all_gather(normed, 'tp', axis=1, tiled=True)]
    pallas_call x0 -> x1, Pallas kernels: none -> 53.6 us  [front(): pl.pallas_call(functools.partial(front_kernel, n_tp), out_shape=[made, ma...]
    all_gather x1, waiting for transfers between devices: 3.23 us -> 21.1 us  [layer(): w_o_full = lax.all_gather(w_o, 'tp', axis=0, tiled=True)]
    dot_general x3 -> x0, matrix products: 16.1 us -> none  [project(): jnp.einsum('rcd,dn->rcn', hidden, weight, preferred_element_type=jnp.floa...]
    concatenate x3 -> x1, other arithmetic: 9.11 us -> 0.7 us  [layer(): bias = jnp.concatenate([b_q, b_k, b_v])[None]]
    convert_element_type x6 -> x0, other arithmetic: 4.81 us -> none  [the longest x2 2.76 us: rms_norm(): return (wide_vals * inv_rms * gain.astype(jnp.float32)).astype(jnp.bfloat16)]
    unnamed x13 -> x19, local copies, waits for them, and re-layouts: 9.32 us -> 9.12 us
  transfers between devices with their start and end apart: 2 -> 1, of which waited for: 2 -> 1; matrix products, arithmetic and copies ran while one was open for 8% -> 0% of each run, Pallas kernels for 12% -> 13%
where the time goes in v2:
time: 241 us; the launch traced here: 240 us
  Pallas kernels  193 us (80%)
  waiting for transfers between devices  21.2 us (9%)
  between operations  14.1 us (6%)
  local copies, waits for them, and re-layouts  10.4 us (4%)
    pallas_call x1, Pallas kernels, tail(): pl.pallas_call(functools.partial(tail_kernel, n_tp), out_shape=jax.ShapeD...  108 us
    pallas_call x1, Pallas kernels, front(): pl.pallas_call(functools.partial(front_kernel, n_tp), out_shape=[made, ma...  53.6 us
    pallas_call x1, Pallas kernels, attention(): pl.pallas_call(functools.partial(attn_kernel, bq, sub, bk), grid_spec=plt...  31.4 us
    all_gather x1, waiting for transfers between devices, layer(): w_o_full = lax.all_gather(w_o, 'tp', axis=0, tiled=True)  21.1 us
    unnamed x19, local copies, waits for them, and re-layouts  9.12 us
  transfers between devices with their start and end apart: 1, of which 1 were waited for; matrix products, arithmetic and copies ran while one was open for 0% of the time, Pallas kernels for 13%

profile of v2, /device:TPU:28, one launch (start us, length us, event | category | flops | bytes accessed | tf_op | source)
XLA Modules:
  0.0 239.9 jit_solution(4627824283401061467)
XLA Ops:
  7.2 0.1 all-gather.2.cloned.1.call-start
  7.3 0.7 reshape.24.g_ref
  8.0 0.7 pad_maximum_fusion
  8.7 0.1 maximum_bitcast_fusion.f_ref
  8.7 0.0 copy-start
  8.7 1.0 copy-done
  9.8 0.0 copy-start.1
  9.8 1.0 copy-done.1
  10.8 0.0 copy-start.2
  10.8 1.0 copy-done.2
  11.9 1.0 copy-done.3
  12.9 0.7 copy-done.4
  13.6 53.6 %front.1 = (bf16[2,1024,128]{2,1,0:T(8,128)(2,1)S(1)}, bf16[2,1024,128]{2,1,0:T(8,128)(2,1)S(1)}, bf16[2,1024,128]{2,1,0:T(8,128)(2,1)S(1)}) custom-call(s32[2]{0:T(128)S(1)} %copy-done.4, bf16[2,64,2048]{2,1,0:T(8,128)(2,1)S(1)} %copy-done.3, bf16[1,2048]{1,0:T(2,128)(2,1)S(1)} %reshape.24.g_ref, f32[1,128]{1,0:T(1,128)S(1)} %maximum_bitcast_fusion.f_ref, ...), custom_call_target="tpu_custom_call" | custom-call | flops 3221225472 | bytes 4194304 | tf_op jit(solution)/shard_map/front/pallas_call | solution.py:361
  67.1 0.0 copy-start.5
  67.1 0.8 copy-done.5
  67.9 0.8 copy-done.6
  68.8 0.8 copy-done.7
  69.6 0.1 all-gather.2.cloned.1.call-update
  69.6 0.0 copy-done.8
  69.6 0.6 reshape.27.g_ref
  70.2 31.4 %attend.1 = (bf16[2,1024,128]{2,1,0:T(8,128)(2,1)}, bf16[2,8192,128]{2,1,0:T(8,128)(2,1)}, bf16[2,8192,128]{2,1,0:T(8,128)(2,1)}) custom-call(s32[2]{0:T(128)} %p_ref.3, s32[2]{0:T(128)} %c_ref.1, bf16[2,1024,128]{2,1,0:T(8,128)(2,1)} %copy-done.5, bf16[2,1024,128]{2,1,0:T(8,128)(2,1)} %copy-done.6, bf16[2,1024,128]{2,1,0:T(8,128)(2,1)} %copy-done.7, ...), custom_call_target="tpu_custom_call" | custom-call | flops 17179869184 | bytes 16777216 | tf_op jit(solution)/shard_map/attend/pallas_call | solution.py:87
  101.6 21.1 %all-gather.2.cloned.1.call-done.wo_hbm = bf16[2048,2048]{1,0:T(8,128)(2,1)} async-done(((bf16[128,2048]{1,0:T(8,128)(2,1)}), bf16[2048,2048]{1,0:T(8,128)(2,1)}) %all-gather.2.cloned.1.call-update) | async-done | bytes 8388624 | tf_op jit(solution)/shard_map/all_gather | solution.py:395
  122.8 108.4 %tail.1 = bf16[2,64,2048]{2,1,0:T(8,128)(2,1)} custom-call(bf16[2,1024,128]{2,1,0:T(8,128)(2,1)} %get-tuple-element.15.o_hbm, bf16[2,64,2048]{2,1,0:T(8,128)(2,1)} %x_ref.3, bf16[1,2048]{1,0:T(2,128)(2,1)} %reshape.27.g_ref, bf16[2048,2048]{1,0:T(8,128)(2,1)} %all-gather.2.cloned.1.call-done.wo_hbm, bf16[688,2048]{1,0:T(8,128)(2,1)} %bitcast.14, ...), custom_call_target="tpu_custom_call" | custom-call | flops 17314086912 | bytes 20971520 | tf_op jit(solution)/shard_map/tail/pallas_call | solution.py:244
  231.1 1.9 copy.23
  (7 shorter events, 0.0 us)
Async XLA Ops:
  7.2 115.6 %all-gather.2.cloned.1.call-start = ((), (), s32[]{:S(2)}) async-start(), calls=%async_computation | async-start | bytes 8912896 | tf_op jit(solution)/shard_map/all_gather | solution.py:395
  8.7 1.0 copy-start
  9.8 1.0 copy-start.1
  10.8 1.0 copy-start.2
  11.9 1.0 copy-start.3
  12.9 0.7 copy-start.4
  13.6 56.1 %copy-start.8 = (bf16[2048]{0:T(1024)(128)(2,1)S(1)}, bf16[2048]{0:T(1024)(128)(2,1)}, u32[]{:S(2)}) copy-start(bf16[2048]{0:T(1024)(128)(2,1)} %param.30) | copy-start | bytes 12292
  67.1 0.8 copy-start.5
  67.9 0.8 copy-start.6
  68.8 0.8 copy-start.7
Sparse Core Ops, SparseCore 0:
  69.7 52.9 all-gather.1

commit v3 on v2

--- a/solution.py
+++ b/solution.py
@@ -109,6 +109,7 @@
     )(prefix, valid, q, kn, vn, kc, vc)
 
 
+CHUNKS = 2
 MESH = pl.DeviceIdType.MESH
 
 
@@ -163,8 +164,11 @@
     for i in (2, 3, 4):
         loads[i].wait()
 
-    def ring_copy(s, way):
-        return remote(rows.at[s, way, 0], rows.at[s + 1, way, 0], ring_send.at[s, way], ring_recv.at[s + 1, way], towards[way])
+    span = n_rows // CHUNKS
+
+    def ring_copy(s, way, h):
+        part = pl.ds(h * span, span)
+        return remote(rows.at[s, way, 0, part], rows.at[s + 1, way, 0, part], ring_send.at[s, way, h], ring_recv.at[s + 1, way, h], towards[way])
 
     def pair_copy(s, way):
         return remote(rows.at[s, way, 0], rows.at[s, way, 1], pair_send.at[s, way], pair_recv.at[s, way], pair)
@@ -172,19 +176,22 @@
     def part_copy(s):
         return remote(part_out.at[s], part_in.at[s], part_send.at[s], part_recv.at[s], pair)
 
-    def sum_copy(s, way):
-        return remote(sums_out.at[s, way], sums_in.at[s + 1, way], sum_send.at[s, way], sum_recv.at[s + 1, way], towards[way])
+    def sum_copy(s, way, h):
+        part = pl.ds(h * span, span)
+        return remote(sums_out.at[s, way, part], sums_in.at[s + 1, way, part], sum_send.at[s, way, h], sum_recv.at[s + 1, way, h], towards[way])
 
     def step(s, _):
-        for way in range(2):
-            @pl.when(s > 0)
-            def _():
-                ring_copy(s - 1, way).wait_recv()
-
-            @pl.when(s < nz - 1)
-            def _():
-                ring_copy(s, way).start()
-
+        for h in range(CHUNKS):
+            for way in range(2):
+                @pl.when(s > 0)
+                def _():
+                    ring_copy(s - 1, way, h).wait_recv()
+
+                @pl.when(s < nz - 1)
+                def _():
+                    ring_copy(s, way, h).start()
+
+        for way in range(2):
             pair_copy(s, way).start()
         for way in range(2):
             pair_copy(s, way).wait_recv()
@@ -200,26 +207,30 @@
         @pl.when(s > 0)
         def _():
             part_copy(s).wait_recv()
-            for way in range(2):
-                @pl.when(s > 1)
-                def _():
-                    sum_copy(s - 1, way).wait_recv()
-                    sums_out[s, way] = (kept[1, way] + part_in[s, way].astype(jnp.float32) + sums_in[s, way].astype(jnp.float32)).astype(jnp.bfloat16)
-
-                @pl.when(s == 1)
-                def _():
-                    sums_out[s, way] = (kept[1, way] + part_in[s, way].astype(jnp.float32)).astype(jnp.bfloat16)
-
-                sum_copy(s, way).start()
+            for h in range(CHUNKS):
+                part = pl.ds(h * span, span)
+                for way in range(2):
+                    @pl.when(s > 1)
+                    def _():
+                        sum_copy(s - 1, way, h).wait_recv()
+                        sums_out[s, way, part] = (kept[1, way, part] + part_in[s, way, part].astype(jnp.float32) + sums_in[s, way, part].astype(jnp.float32)).astype(jnp.bfloat16)
+
+                    @pl.when(s == 1)
+                    def _():
+                        sums_out[s, way, part] = (kept[1, way, part] + part_in[s, way, part].astype(jnp.float32)).astype(jnp.bfloat16)
+
+                    sum_copy(s, way, h).start()
         return 0
 
     lax.fori_loop(0, nz, step, 0)
 
     part_copy(0).wait_recv()
-    for way in range(2):
-        sum_copy(nz - 1, way).wait_recv()
-        total = kept[0, way] + part_in[0, way].astype(jnp.float32) + sums_in[nz, way].astype(jnp.float32)
-        out_ref[way] = (x1[way].astype(jnp.float32) + total.astype(jnp.bfloat16).astype(jnp.float32)).astype(jnp.bfloat16)
+    for h in range(CHUNKS):
+        part = pl.ds(h * span, span)
+        for way in range(2):
+            sum_copy(nz - 1, way, h).wait_recv()
+            total = kept[0, way, part] + part_in[0, way, part].astype(jnp.float32) + sums_in[nz, way, part].astype(jnp.float32)
+            out_ref[way, part] = (x1[way, part].astype(jnp.float32) + total.astype(jnp.bfloat16).astype(jnp.float32)).astype(jnp.bfloat16)
 
     for c in sends:
         c.wait_send()
@@ -228,9 +239,11 @@
         for way in range(2):
             pair_copy(s, way).wait_send()
             if s < nz - 1:
-                ring_copy(s, way).wait_send()
+                for h in range(CHUNKS):
+                    ring_copy(s, way, h).wait_send()
             if s > 0:
-                sum_copy(s, way).wait_send()
+                for h in range(CHUNKS):
+                    sum_copy(s, way, h).wait_send()
 
 
 def tail(n_tp, o, x, gain, w_o, w_gate, w_up, w_down):
@@ -261,8 +274,8 @@
             pltpu.VMEM((nz, 2, n_rows, width), bf),
             pltpu.VMEM((2, 2, n_rows, width), jnp.float32),
             dma((5,)), dma((n_tp,)), dma((n_tp,)),
-            dma((nz, 2)), dma((nz, 2)), dma((nz, 2)), dma((nz, 2)),
-            dma((nz, 2)), dma((nz + 1, 2)), dma((nz,)), dma((nz,)),
+            dma((nz, 2, CHUNKS)), dma((nz, 2, CHUNKS)), dma((nz, 2)), dma((nz, 2)),
+            dma((nz, 2, CHUNKS)), dma((nz + 1, 2, CHUNKS)), dma((nz,)), dma((nz,)),
         ],
         compiler_params=pltpu.CompilerParams(vmem_limit_bytes=62 * 2**20, collective_id=1, has_side_effects=True),
         cost_estimate=pl.CostEstimate(flops=6 * n_tp * n_req * n_rows * width * ffn, bytes_accessed=20 * 2**20, transcendentals=0),
@@ -270,7 +283,8 @@
     )(o, x, gain.reshape(1, width), w_o, w_gate, w_up, w_down)
 
 
-def front_kernel(n_tp, p_ref, x_ref, g_ref, f_ref, b_ref, wq_hbm, wk_hbm, wv_hbm, q_ref, k_ref, v_ref, w, rows, load_sem, ring_send, ring_recv, pair_send, pair_recv):
+def front_kernel(n_tp, n_dp, p_ref, x_ref, g_ref, f_ref, b_ref, wq_hbm, wk_hbm, wv_hbm, wo_hbm, q_ref, k_ref, v_ref, all_hbm,
+                 w, rows, wo, load_sem, ring_send, ring_recv, pair_send, pair_recv, a_send, a_recv, b_send, b_recv, c_send, c_recv):
     nz = n_tp // 2
     me = lax.axis_index("tp")
     core = lax.rem(me, 2)
@@ -283,35 +297,97 @@
     d = q_ref.shape[-1]
 
     loads = [pltpu.make_async_copy(s, w.at[:, pl.ds(i * d, d)], load_sem.at[i]) for i, s in enumerate((wq_hbm, wk_hbm, wv_hbm))]
+    own_load = pltpu.make_async_copy(wo_hbm, wo, load_sem.at[3])
+    own_load.start()
     for c in loads:
         c.start()
 
+    group = lax.axis_index("dp")
     barrier = pltpu.get_barrier_semaphore()
     for there in (up, down, pair):
         pl.semaphore_signal(barrier, inc=1, device_id={"tp": there}, device_id_type=MESH)
+    for k in range(1, n_dp):
+        pl.semaphore_signal(barrier, inc=1, device_id={"dp": lax.rem(group + k, n_dp)}, device_id_type=MESH)
 
     wide = x_ref[...].astype(jnp.float32)
     inv = lax.rsqrt(jnp.mean(wide * wide, axis=-1, keepdims=True) + NORM_EPS)
     rows[0, :, 0] = (wide * inv * g_ref[...].astype(jnp.float32)).astype(jnp.bfloat16)
-    pl.semaphore_wait(barrier, 3)
-
-    def ring_copy(s, way):
-        return remote(rows.at[s, way, 0], rows.at[s + 1, way, 0], ring_send.at[s, way], ring_recv.at[s + 1, way], towards[way])
+    pl.semaphore_wait(barrier, 2 + n_dp)
+
+    n_own = wo.shape[0]
+    share = n_own // n_dp
+    reach = (nz // 2, (nz - 1) // 2)
+
+    def home_rows(s, way, part, count):
+        home = lax.rem(chip + (nz - s if way == 0 else s), nz) * 2 + core
+        return pl.ds(pl.multiple_of(home * n_own + part * share, 8), count)
+
+    def a_copy(s, way, src=None):
+        at = home_rows(s, way, group, share)
+        return remote(all_hbm.at[at] if src is None else src, all_hbm.at[at], a_send.at[s, way], a_recv.at[s + 1, way], towards[way])
+
+    def b_copy(s, way, k):
+        at = home_rows(s, way, group, share)
+        return pltpu.make_async_remote_copy(src_ref=all_hbm.at[at], dst_ref=all_hbm.at[at], send_sem=b_send.at[s, way, k], recv_sem=b_recv.at[s, way, k],
+                                            device_id={"dp": lax.rem(group + k, n_dp)}, device_id_type=MESH)
+
+    def b_wait(s, way, k):
+        at = home_rows(s, way, lax.rem(group + n_dp - k, n_dp), share)
+        pltpu.make_async_remote_copy(src_ref=all_hbm.at[at], dst_ref=all_hbm.at[at], send_sem=b_send.at[s, way, k], recv_sem=b_recv.at[s, way, k],
+                                     device_id={"dp": lax.rem(group + k, n_dp)}, device_id_type=MESH).wait_recv()
+
+    def c_copy(s, way, src=None):
+        at = home_rows(s, way, 0, n_own)
+        return remote(all_hbm.at[at] if src is None else src, all_hbm.at[at], c_send.at[s, way], c_recv.at[s, way], pair)
+
+    def c_wait(s, way):
+        home = lax.rem(chip + (nz - s if way == 0 else s), nz) * 2 + 1 - core
+        at = pl.ds(pl.multiple_of(home * n_own, 8), n_own)
+        remote(all_hbm.at[at], all_hbm.at[at], c_send.at[s, way], c_recv.at[s, way], pair).wait_recv()
+
+    own_load.wait()
+    own_share = wo.at[pl.ds(pl.multiple_of(group * share, 8), share)]
+    own_store = pltpu.make_async_copy(wo, all_hbm.at[home_rows(0, 0, 0, n_own)], load_sem.at[3])
+    own_store.start()
+    c_copy(0, 0, wo).start()
+
+    span = n_rows // CHUNKS
+
+    def ring_copy(s, way, h):
+        part = pl.ds(h * span, span)
+        return remote(rows.at[s, way, 0, part], rows.at[s + 1, way, 0, part], ring_send.at[s, way, h], ring_recv.at[s + 1, way, h], towards[way])
 
     def pair_copy(s, way):
         return remote(rows.at[s, way, 0], rows.at[s, way, 1], pair_send.at[s, way], pair_recv.at[s, way], pair)
 
     def step(s, _):
-        for way in range(2):
-            @pl.when(s > 0)
+        for h in range(CHUNKS):
+            for way in range(2):
+                @pl.when(s > 0)
+                def _():
+                    ring_copy(s - 1, way, h).wait_recv()
+
+                @pl.when(s < nz - 1)
+                def _():
+                    ring_copy(s, way, h).start()
+
+        for way in range(2):
+            pair_copy(s, way).start()
+
+            @pl.when(s == 0)
             def _():
-                ring_copy(s - 1, way).wait_recv()
-
-            @pl.when(s < nz - 1)
+                a_copy(0, way, own_share).start()
+
+            @pl.when((s > 0) & (s <= reach[way]))
             def _():
-                ring_copy(s, way).start()
-
-            pair_copy(s, way).start()
+                a_copy(s - 1, way).wait_recv()
+
+                @pl.when(s < reach[way])
+                def _():
+                    a_copy(s, way).start()
+
+                for k in range(1, n_dp):
+                    b_copy(s, way, k).start()
 
         @pl.when(s == 0)
         def _():
@@ -341,14 +417,33 @@
         return 0
 
     lax.fori_loop(0, nz, step, 0)
+
+    pieces = [(s, way) for s in range(1, nz // 2 + 1) for way in range(2) if s <= reach[way]]
+    for s, way in pieces:
+        for k in range(1, n_dp):
+            b_wait(s, way, k)
+        c_copy(s, way).start()
+    own_store.wait()
+    c_copy(0, 0, wo).wait_send()
+    c_wait(0, 0)
+    for way in range(2):
+        a_copy(0, way, own_share).wait_send()
+    for s, way in pieces:
+        c_wait(s, way)
+        c_copy(s, way).wait_send()
+        for k in range(1, n_dp):
+            b_copy(s, way, k).wait_send()
+        if s < reach[way]:
+            a_copy(s, way).wait_send()
     for s in range(nz):
         for way in range(2):
             pair_copy(s, way).wait_send()
             if s < nz - 1:
-                ring_copy(s, way).wait_send()
-
-
-def front(n_tp, x, gain, prefix, freq, bias, w_q, w_k, w_v):
+                for h in range(CHUNKS):
+                    ring_copy(s, way, h).wait_send()
+
+
+def front(n_tp, n_dp, x, gain, prefix, freq, bias, w_q, w_k, w_v, w_o):
     n_req, n_rows, width = x.shape
     d = w_q.shape[1]
     nz = n_tp // 2
@@ -359,19 +454,21 @@
     dma = pltpu.SemaphoreType.DMA
     made = jax.ShapeDtypeStruct((n_req, n_tok, d), bf)
     return pl.pallas_call(
-        functools.partial(front_kernel, n_tp),
-        out_shape=[made, made, made],
-        in_specs=[pl.BlockSpec(memory_space=pltpu.SMEM), vm, vm, vm, vm, any_spec, any_spec, any_spec],
-        out_specs=[vm, vm, vm],
+        functools.partial(front_kernel, n_tp, n_dp),
+        out_shape=[made, made, made, jax.ShapeDtypeStruct((n_tp * d, width), bf)],
+        in_specs=[pl.BlockSpec(memory_space=pltpu.SMEM), vm, vm, vm, vm, any_spec, any_spec, any_spec, any_spec],
+        out_specs=[vm, vm, vm, any_spec],
         scratch_shapes=[
             pltpu.VMEM((width, 3 * d), bf),
             pltpu.VMEM((nz, 2, 2, n_rows, width), bf),
-            dma((3,)), dma((nz, 2)), dma((nz, 2)), dma((nz, 2)), dma((nz, 2)),
+            pltpu.VMEM(w_o.shape, bf),
+            dma((4,)), dma((nz, 2, CHUNKS)), dma((nz, 2, CHUNKS)), dma((nz, 2)), dma((nz, 2)),
+            dma((nz, 2)), dma((nz, 2)), dma((nz, 2, n_dp)), dma((nz, 2, n_dp)), dma((nz, 2)), dma((nz, 2)),
         ],
         compiler_params=pltpu.CompilerParams(vmem_limit_bytes=40 * 2**20, collective_id=2, has_side_effects=True),
         cost_estimate=pl.CostEstimate(flops=6 * n_req * n_tok * width * d, bytes_accessed=4 * 2**20, transcendentals=0),
         name="front",
-    )(prefix, x, gain.reshape(1, width), freq, bias, w_q, w_k, w_v)
+    )(prefix, x, gain.reshape(1, width), freq, bias, w_q, w_k, w_v, w_o)
 
 
 def solution(mesh):
@@ -390,9 +487,7 @@
         freq = ROPE_THETA ** (-(half * 2.0) / head_dim)
         freq = jnp.concatenate([freq, freq])[None]
         bias = jnp.concatenate([b_q, b_k, b_v])[None]
-        q, k, v = front(n_tp, x_rows, g_attn, prefix, freq, bias, w_q, w_k, w_v)
-        w_o, q = lax.optimization_barrier((w_o, q))
-        w_o_full = lax.all_gather(w_o, "tp", axis=0, tiled=True)
+        q, k, v, w_o_full = front(n_tp, mesh.shape["dp"], x_rows, g_attn, prefix, freq, bias, w_q, w_k, w_v, w_o)
         flat = (n_req, -1, head_dim)
         o, k_out, v_out = attention(q, k, v, k_cache.reshape(flat), v_cache.reshape(flat), prefix, valid)
         out = tail(n_tp, o, x_rows, g_mlp, w_o_full, w_gate.T, w_up.T, w_down)

time: 241 us -> 231 us (0.959)
  waiting for transfers between devices: 21.2 us -> 0 us
  Pallas kernels: 193 us -> 212 us
  between operations: 14.1 us -> 0.67 us
  local copies, waits for them, and re-layouts: 10.4 us -> 14.7 us
    all_gather x1 -> x0, waiting for transfers between devices: 21.1 us -> none  [layer(): w_o_full = lax.all_gather(w_o, 'tp', axis=0, tiled=True)]
    pallas_call x1, Pallas kernels: 53.6 us -> 72.6 us  [front(): pl.pallas_call(functools.partial(front_kernel, n_tp, n_dp), out_shape=[ma...]
    unnamed x19 -> x23, local copies, waits for them, and re-layouts: 9.12 us -> 13.4 us
  transfers between devices with their start and end apart: 1 -> 0, of which waited for: 1 -> 0; matrix products, arithmetic and copies ran while one was open for 0% -> 0% of each run, Pallas kernels for 13% -> 0%
where the time goes in v3:
time: 231 us; the launch traced here: 228 us
  Pallas kernels  212 us (92%)
  local copies, waits for them, and re-layouts  14.7 us (6%)
    pallas_call x1, Pallas kernels, tail(): pl.pallas_call(functools.partial(tail_kernel, n_tp), out_shape=jax.ShapeD...  108 us
    pallas_call x1, Pallas kernels, front(): pl.pallas_call(functools.partial(front_kernel, n_tp, n_dp), out_shape=[ma...  72.6 us
    pallas_call x1, Pallas kernels, attention(): pl.pallas_call(functools.partial(attn_kernel, bq, sub, bk), grid_spec=plt...  31 us
    unnamed x23, local copies, waits for them, and re-layouts  13.4 us

profile of v3, /device:TPU:28, one launch (start us, length us, event | category | flops | bytes accessed | tf_op | source)
XLA Modules:
  0.0 227.7 jit_solution(14933433428750399777)
XLA Ops:
  0.6 0.7 reshape.24.g_ref
  1.3 0.7 pad_maximum_fusion
  2.0 0.1 maximum_bitcast_fusion.f_ref
  2.1 0.0 copy-start
  2.1 1.0 copy-done
  3.2 0.0 copy-start.1
  3.2 1.0 copy-done.1
  4.2 0.0 copy-start.2
  4.2 1.0 copy-done.2
  5.2 0.0 copy-start.3
  5.3 1.0 copy-done.3
  6.3 1.0 copy-done.4
  7.3 0.7 copy-done.5
  8.0 72.6 %front.1 = (bf16[2,1024,128]{2,1,0:T(8,128)(2,1)S(1)}, bf16[2,1024,128]{2,1,0:T(8,128)(2,1)S(1)}, bf16[2,1024,128]{2,1,0:T(8,128)(2,1)S(1)}, bf16[2048,2048]{1,0:T(8,128)(2,1)S(1)}) custom-call(s32[2]{0:T(128)S(1)} %copy-done.5, bf16[2,64,2048]{2,1,0:T(8,128)(2,1)S(1)} %copy-done.4, bf16[1,2048]{1,0:T(2,128)(2,1)S(1)} %reshape.24.g_ref, ...), custom_call_target="tpu_custom_call" | custom-call | flops 3221225472 | bytes 4194304 | tf_op jit(solution)/shard_map/front/pallas_call | solution.py:456
  80.6 0.0 copy-start.6
  80.6 3.2 %copy-done.6 = bf16[2048,2048]{1,0:T(8,128)(2,1)} copy-done((bf16[2048,2048]{1,0:T(8,128)(2,1)}, bf16[2048,2048]{1,0:T(8,128)(2,1)S(1)}, u32[]{:S(2)}) %copy-start.6) | copy-done | bytes 8388632
  83.8 0.8 copy-done.7
  84.6 0.8 copy-done.8
  85.5 0.8 copy-done.9
  86.3 31.0 %attend.1 = (bf16[2,1024,128]{2,1,0:T(8,128)(2,1)}, bf16[2,8192,128]{2,1,0:T(8,128)(2,1)}, bf16[2,8192,128]{2,1,0:T(8,128)(2,1)}) custom-call(s32[2]{0:T(128)} %p_ref.3, s32[2]{0:T(128)} %c_ref.1, bf16[2,1024,128]{2,1,0:T(8,128)(2,1)} %copy-done.7, bf16[2,1024,128]{2,1,0:T(8,128)(2,1)} %copy-done.8, bf16[2,1024,128]{2,1,0:T(8,128)(2,1)} %copy-done.9, ...), custom_call_target="tpu_custom_call" | custom-call | flops 17179869184 | bytes 16777216 | tf_op jit(solution)/shard_map/attend/pallas_call | solution.py:87
  117.3 0.0 copy-done.10
  117.3 0.6 reshape.27.g_ref
  117.9 107.9 %tail.1 = bf16[2,64,2048]{2,1,0:T(8,128)(2,1)} custom-call(bf16[2,1024,128]{2,1,0:T(8,128)(2,1)} %get-tuple-element.13.o_hbm, bf16[2,64,2048]{2,1,0:T(8,128)(2,1)} %x_ref.3, bf16[1,2048]{1,0:T(2,128)(2,1)} %reshape.27.g_ref, bf16[2048,2048]{1,0:T(8,128)(2,1)} %copy-done.6, bf16[688,2048]{1,0:T(8,128)(2,1)} %bitcast.14, bf16[688,2048]{1,0:T(8,128)(2,1)} %bitcast.15, ...), custom_call_target="tpu_custom_call" | custom-call | flops 17314086912 | bytes 20971520 | tf_op jit(solution)/shard_map/tail/pallas_call | solution.py:257
  225.9 1.9 copy.23
  (8 shorter events, 0.0 us)
Async XLA Ops:
  2.1 1.0 copy-start
  3.2 1.0 copy-start.1
  4.2 1.0 copy-start.2
  5.2 1.0 copy-start.3
  6.3 1.0 copy-start.4
  7.3 0.7 copy-start.5
  80.6 3.2 %copy-start.6 = (bf16[2048,2048]{1,0:T(8,128)(2,1)}, bf16[2048,2048]{1,0:T(8,128)(2,1)S(1)}, u32[]{:S(2)}) copy-start(bf16[2048,2048]{1,0:T(8,128)(2,1)S(1)} %get-tuple-element.14.wo_hbm) | copy-start | bytes 25165828
  83.8 0.8 copy-start.7
  84.6 0.8 copy-start.8
  85.5 0.8 copy-start.9
  86.3 31.0 %copy-start.10 = (bf16[2048]{0:T(1024)(128)(2,1)S(1)}, bf16[2048]{0:T(1024)(128)(2,1)}, u32[]{:S(2)}) copy-start(bf16[2048]{0:T(1024)(128)(2,1)} %param.30) | copy-start | bytes 12292

commit v4 on v3

v4 whole, which is shorter than its diff:
```python
import functools
import math

import jax
import jax.numpy as jnp
from jax import lax
from jax.experimental import pallas as pl
from jax.experimental.pallas import tpu as pltpu
from jax.sharding import PartitionSpec as P

ROPE_THETA = 1.0e6
NORM_EPS = 1.0e-6


CHUNKS = 2
MESH = pl.DeviceIdType.MESH


def remote(src, dst, send, recv, target):
    return pltpu.make_async_remote_copy(src_ref=src, dst_ref=dst, send_sem=send, recv_sem=recv, device_id={"tp": target}, device_id_type=MESH)


def tail_kernel(n_tp, o_all, x_ref, g_ref, wo_hbm, wg_hbm, wu_hbm, wd_hbm, out_ref,
                wo, wg, wu, wd, x1, rows, sums_in, sums_out, part_in, part_out, kept,
                load_sem, ring_send, ring_recv, pair_send, pair_recv, sum_send, sum_recv, part_send, part_recv):
    nz = n_tp // 2
    me = lax.axis_index("tp")
    core = lax.rem(me, 2)
    chip = me // 2
    up = lax.rem(chip + 1, nz) * 2 + core
    down = lax.rem(chip + nz - 1, nz) * 2 + core
    pair = chip * 2 + 1 - core
    towards = (up, down)
    n_req, n_rows, width = x_ref.shape

    loads = [pltpu.make_async_copy(s, t, load_sem.at[i]) for i, (s, t) in enumerate(((wo_hbm, wo), (wg_hbm, wg), (wu_hbm, wu), (wd_hbm, wd)))]
    for c in loads:
        c.start()

    barrier = pltpu.get_barrier_semaphore()
    for there in (up, down, pair):
        pl.semaphore_signal(barrier, inc=1, device_id={"tp": there}, device_id_type=MESH)

    loads[0].wait()
    mixed = jnp.dot(o_all[...].reshape(n_req * n_rows, width), wo[...], preferred_element_type=jnp.float32).astype(jnp.bfloat16)
    resid = (x_ref[...].reshape(n_req * n_rows, width).astype(jnp.float32) + mixed.astype(jnp.float32)).astype(jnp.bfloat16)
    x1[...] = resid.reshape(x1.shape)
    wide = resid.astype(jnp.float32)
    inv = lax.rsqrt(jnp.mean(wide * wide, axis=-1, keepdims=True) + NORM_EPS)
    normed = (wide * inv * g_ref[...].astype(jnp.float32)).astype(jnp.bfloat16)
    pl.semaphore_wait(barrier, 3)
    rows[0, :, 0] = normed.reshape(n_req, n_rows, width)

    for i in (1, 2, 3):
        loads[i].wait()

    span = n_rows // CHUNKS

    def ring_copy(s, way, h):
        part = pl.ds(h * span, span)
        return remote(rows.at[s, way, 0, part], rows.at[s + 1, way, 0, part], ring_send.at[s, way, h], ring_recv.at[s + 1, way, h], towards[way])

    def pair_copy(s, way):
        return remote(rows.at[s, way, 0], rows.at[s, way, 1], pair_send.at[s, way], pair_recv.at[s, way], pair)

    def part_copy(s):
        return remote(part_out.at[s], part_in.at[s], part_send.at[s], part_recv.at[s], pair)

    def sum_copy(s, way, h):
        part = pl.ds(h * span, span)
        return remote(sums_out.at[s, way, part], sums_in.at[s + 1, way, part], sum_send.at[s, way, h], sum_recv.at[s + 1, way, h], towards[way])

    def step(s, _):
        for h in range(CHUNKS):
            for way in range(2):
                @pl.when(s > 0)
                def _():
                    ring_copy(s - 1, way, h).wait_recv()

                @pl.when(s < nz - 1)
                def _():
                    ring_copy(s, way, h).start()

        for way in range(2):
            pair_copy(s, way).start()
        for way in range(2):
            pair_copy(s, way).wait_recv()
        lhs = rows[s].reshape(4 * n_rows, width)
        gate = lax.dot_general(lhs, wg[...], (((1,), (1,)), ((), ())), preferred_element_type=jnp.float32)
        lift = lax.dot_general(lhs, wu[...], (((1,), (1,)), ((), ())), preferred_element_type=jnp.float32)
        act = (jax.nn.silu(gate) * lift).astype(jnp.bfloat16)
        part = jnp.dot(act, wd[...], preferred_element_type=jnp.float32).reshape(2, 2, n_rows, width)
        part_out[s] = part[:, 1].astype(jnp.bfloat16)
        part_copy(s).start()
        kept[jnp.minimum(s, 1)] = part[:, 0]

        @pl.when(s > 0)
        def _():
            part_copy(s).wait_recv()
            for h in range(CHUNKS):
                part = pl.ds(h * span, span)
                for way in range(2):
                    @pl.when(s > 1)
                    def _():
                        sum_copy(s - 1, way, h).wait_recv()
                        sums_out[s, way, part] = (kept[1, way, part] + part_in[s, way, part].astype(jnp.float32) + sums_in[s, way, part].astype(jnp.float32)).astype(jnp.bfloat16)

                    @pl.when(s == 1)
                    def _():
                        sums_out[s, way, part] = (kept[1, way, part] + part_in[s, way, part].astype(jnp.float32)).astype(jnp.bfloat16)

                    sum_copy(s, way, h).start()
        return 0

    lax.fori_loop(0, nz, step, 0)

    part_copy(0).wait_recv()
    for h in range(CHUNKS):
        part = pl.ds(h * span, span)
        for way in range(2):
            sum_copy(nz - 1, way, h).wait_recv()
            total = kept[0, way, part] + part_in[0, way, part].astype(jnp.float32) + sums_in[nz, way, part].astype(jnp.float32)
            out_ref[way, part] = (x1[way, part].astype(jnp.float32) + total.astype(jnp.bfloat16).astype(jnp.float32)).astype(jnp.bfloat16)

    for s in range(nz):
        part_copy(s).wait_send()
        for way in range(2):
            pair_copy(s, way).wait_send()
            if s < nz - 1:
                for h in range(CHUNKS):
                    ring_copy(s, way, h).wait_send()
            if s > 0:
                for h in range(CHUNKS):
                    sum_copy(s, way, h).wait_send()


def tail(n_tp, o, x, gain, w_o, w_gate, w_up, w_down):
    n_req, n_rows, width = x.shape
    ffn = w_gate.shape[0]
    nz = n_tp // 2
    bf = jnp.bfloat16
    any_spec = pl.BlockSpec(memory_space=pl.ANY)
    vm = pl.BlockSpec(memory_space=pltpu.VMEM)
    dma = pltpu.SemaphoreType.DMA
    return pl.pallas_call(
        functools.partial(tail_kernel, n_tp),
        out_shape=jax.ShapeDtypeStruct(x.shape, x.dtype),
        in_specs=[vm, vm, vm, any_spec, any_spec, any_spec, any_spec],
        out_specs=vm,
        scratch_shapes=[
            pltpu.VMEM(w_o.shape, bf),
            pltpu.VMEM(w_gate.shape, bf),
            pltpu.VMEM(w_up.shape, bf),
            pltpu.VMEM(w_down.shape, bf),
            pltpu.VMEM((n_req, n_rows, width), bf),
            pltpu.VMEM((nz, 2, 2, n_rows, width), bf),
            pltpu.VMEM((nz + 1, 2, n_rows, width), bf),
            pltpu.VMEM((nz, 2, n_rows, width), bf),
            pltpu.VMEM((nz, 2, n_rows, width), bf),
            pltpu.VMEM((nz, 2, n_rows, width), bf),
            pltpu.VMEM((2, 2, n_rows, width), jnp.float32),
            dma((4,)),
            dma((nz, 2, CHUNKS)), dma((nz, 2, CHUNKS)), dma((nz, 2)), dma((nz, 2)),
            dma((nz, 2, CHUNKS)), dma((nz + 1, 2, CHUNKS)), dma((nz,)), dma((nz,)),
        ],
        compiler_params=pltpu.CompilerParams(vmem_limit_bytes=62 * 2**20, collective_id=1, has_side_effects=True),
        cost_estimate=pl.CostEstimate(flops=6 * n_tp * n_req * n_rows * width * ffn, bytes_accessed=20 * 2**20, transcendentals=0),
        name="tail",
    )(o, x, gain.reshape(1, width), w_o, w_gate, w_up, w_down)


NEG = -1.0e30
KEY_BLOCKS = 4


def front_kernel(n_tp, n_dp, p_ref, c_ref, x_ref, g_ref, f_ref, b_ref, wq_hbm, wk_hbm, wv_hbm, wo_hbm, kc_hbm, vc_hbm,
                 o_all, kn_ref, vn_ref, all_hbm, ko_hbm, vo_hbm,
                 w, rows, wo, kc, vc, vext, q_abs, vn_ext, m_abs, acc_abs, q_now, m_now, acc_now, o_v,
                 load_sem, cache_sem, ring_send, ring_recv, pair_send, pair_recv, a_send, a_recv, b_send, b_recv, c_send, c_recv, o_send, o_recv):
    nz = n_tp // 2
    me = lax.axis_index("tp")
    core = lax.rem(me, 2)
    chip = me // 2
    group = lax.axis_index("dp")
    up = lax.rem(chip + 1, nz) * 2 + core
    down = lax.rem(chip + nz - 1, nz) * 2 + core
    pair = chip * 2 + 1 - core
    towards = (up, down)
    n_req, n_rows, width = x_ref.shape
    d = q_abs.shape[-1]
    two = 2 * n_rows
    old = vext.shape[1]
    bf, f32 = jnp.bfloat16, jnp.float32

    own_load = pltpu.make_async_copy(wo_hbm, wo, load_sem.at[3])
    own_load.start()
    loads = [pltpu.make_async_copy(s, w.at[:, pl.ds(i * d, d)], load_sem.at[i]) for i, s in enumerate((wq_hbm, wk_hbm, wv_hbm))]
    for c in loads:
        c.start()
    cache_in = [pltpu.make_async_copy(kc_hbm, kc, cache_sem.at[0]), pltpu.make_async_copy(vc_hbm, vc, cache_sem.at[1])]
    cache_out = [pltpu.make_async_copy(kc, ko_hbm, cache_sem.at[2]), pltpu.make_async_copy(vc, vo_hbm, cache_sem.at[3])]
    for c in cache_in:
        c.start()

    barrier = pltpu.get_barrier_semaphore()
    for k in range(1, n_tp):
        pl.semaphore_signal(barrier, inc=1, device_id={"tp": lax.rem(me + k, n_tp)}, device_id_type=MESH)
    for k in range(1, n_dp):
        pl.semaphore_signal(barrier, inc=1, device_id={"dp": lax.rem(group + k, n_dp)}, device_id_type=MESH)

    wide = x_ref[...].astype(f32)
    inv = lax.rsqrt(jnp.mean(wide * wide, axis=-1, keepdims=True) + NORM_EPS)
    rows[0, :, 0] = (wide * inv * g_ref[...].astype(f32)).astype(bf)
    pl.semaphore_wait(barrier, n_tp + n_dp - 2)

    span = n_rows // CHUNKS

    def ring_copy(s, way, h):
        part = pl.ds(h * span, span)
        return remote(rows.at[s, way, 0, part], rows.at[s + 1, way, 0, part], ring_send.at[s, way, h], ring_recv.at[s + 1, way, h], towards[way])

    def pair_copy(s, way):
        return remote(rows.at[s, way, 0], rows.at[s, way, 1], pair_send.at[s, way], pair_recv.at[s, way], pair)

    n_own = wo.shape[0]
    share = n_own // n_dp
    reach = (nz // 2, (nz - 1) // 2)

    def away(s, way):
        return lax.rem(chip + (nz - s if way == 0 else s), nz)

    def home_rows(s, way, part, count):
        return pl.ds(pl.multiple_of((away(s, way) * 2 + core) * n_own + part * share, 8), count)

    def a_copy(s, way, src=None):
        at = home_rows(s, way, group, share)
        return remote(all_hbm.at[at] if src is None else src, all_hbm.at[at], a_send.at[s, way], a_recv.at[s + 1, way], towards[way])

    def b_copy(s, way, k, owner=None):
        at = home_rows(s, way, group if owner is None else owner, share)
        return pltpu.make_async_remote_copy(src_ref=all_hbm.at[at], dst_ref=all_hbm.at[at], send_sem=b_send.at[s, way, k], recv_sem=b_recv.at[s, way, k],
                                            device_id={"dp": lax.rem(group + k, n_dp)}, device_id_type=MESH)

    def c_copy(s, way, src=None):
        at = home_rows(s, way, 0, n_own)
        return remote(all_hbm.at[at] if src is None else src, all_hbm.at[at], c_send.at[s, way], c_recv.at[s, way], pair)

    def c_wait(s, way):
        at = pl.ds(pl.multiple_of((away(s, way) * 2 + 1 - core) * n_own, 8), n_own)
        remote(all_hbm.at[at], all_hbm.at[at], c_send.at[s, way], c_recv.at[s, way], pair).wait_recv()

    for h in range(CHUNKS):
        for way in range(2):
            ring_copy(0, way, h).start()
    for way in range(2):
        pair_copy(0, way).start()
    own_load.wait()
    own_share = wo.at[pl.ds(pl.multiple_of(group * share, 8), share)]
    own_store = pltpu.make_async_copy(wo, all_hbm.at[home_rows(0, 0, 0, n_own)], load_sem.at[3])
    for way in range(2):
        a_copy(0, way, own_share).start()
    own_store.start()
    c_copy(0, 0, wo).start()

    for i in range(2):
        cache_in[i].wait()
        cache_out[i].start()
    for c in cache_out:
        c.wait()
    tile = 1024
    for r in range(n_req):
        def tidy(t, _):
            at = pl.ds(pl.multiple_of(t * tile, tile), tile)
            there = lax.broadcasted_iota(jnp.int32, (tile, d), 0) + t * tile < p_ref[r]
            first = kc[r, 0:16, :].astype(f32)[0:1]
            kc[r, at, :] = jnp.where(there, kc[r, at, :].astype(f32), first).astype(bf)
            vext[r, at, :d] = jnp.where(there, vc[r, at, :].astype(f32), 0.0).astype(bf)
            vext[r, at, d:] = jnp.where(there, 1.0, 0.0).astype(bf)
            return 0

        lax.fori_loop(0, old // tile, tidy, 0)
    vn_ext[:, :, d:] = jnp.ones((n_req, vn_ext.shape[1], d), bf)
    for c in loads:
        c.wait()

    def tick(s):
        @pl.when(s < nz)
        def _():
            for h in range(CHUNKS):
                for way in range(2):
                    ring_copy(s - 1, way, h).wait_recv()

                    @pl.when(s < nz - 1)
                    def _():
                        ring_copy(s, way, h).start()

            for way in range(2):
                pair_copy(s, way).start()

                @pl.when(s <= reach[way])
                def _():
                    a_copy(s - 1, way).wait_recv()

                    @pl.when(s < reach[way])
                    def _():
                        a_copy(s, way).start()

                    for k in range(1, n_dp):
                        b_copy(s, way, k).start()

    scale2 = (d ** -0.5) * math.log2(math.e)
    block = old // KEY_BLOCKS
    nt = (((1,), (1,)), ((), ()))

    def flash(s, m_prev, acc, vals):
        m_new = jnp.maximum(m_prev, jnp.max(s, axis=1, keepdims=True))
        a = jnp.exp2((m_prev - m_new) * scale2)
        p = jnp.exp2((s - m_new[:, :1]) * scale2).astype(bf)
        return m_new, acc * jnp.concatenate([a, a], axis=1) + jnp.dot(p, vals, preferred_element_type=f32)

    tick(1)

    def two_steps(k, _):
        for t in range(2):
            for way in range(2):
                pair_copy(2 * k + t, way).wait_recv()
        lhs = rows[pl.ds(2 * k, 2)].reshape(8 * n_rows, width)
        total = jnp.dot(lhs, w[...], preferred_element_type=f32)
        got = (total + b_ref[...].astype(f32)).astype(bf)
        sign = jnp.where(lax.broadcasted_iota(jnp.int32, (n_rows, d), 1) < d // 2, -1.0, 1.0)

        def places():
            for t in range(2):
                for way in range(2):
                    for other in range(2):
                        off = pl.multiple_of((away(2 * k + t, way) * 2 + (core if other == 0 else 1 - core)) * n_rows, n_rows)
                        yield t, way, other, off

        for t, way, other, off in places():
            at = pl.ds(off, n_rows)
            spot = (lax.broadcasted_iota(jnp.int32, (n_rows, d), 0) + (p_ref[way] + off)).astype(f32)
            angle = spot * f_ref[...]
            cos_t = jnp.cos(angle)
            sin_t = jnp.sin(angle) * sign
            i = ((t * 2 + way) * 2 + other) * n_rows
            mine = got[i:i + n_rows]
            turned = []
            for part in (mine[:, :d], mine[:, d:2 * d]):
                part = part.astype(f32)
                turned.append((part * cos_t + pltpu.roll(part, d // 2, 1) * sin_t).astype(bf))
            q_abs[way, at, :] = turned[0]
            q_now[way, pl.ds(t * two + other * n_rows, n_rows), :] = turned[0]
            kn_ref[way, at, :] = turned[1]
            vn_ref[way, at, :] = mine[:, 2 * d:]
            vn_ext[way, at, :d] = mine[:, 2 * d:]

        m_now[...] = jnp.full_like(m_now, NEG)
        acc_now[...] = jnp.zeros_like(acc_now)

        def keys(j, _):
            at = pl.ds(pl.multiple_of(j * block, block), block)
            for u in range(2):
                for way in range(2):
                    sl = pl.ds(u * two, two)
                    s = lax.dot_general(q_now[way, sl, :], kc[way, at, :], nt, preferred_element_type=f32)
                    m_now[way, sl, :], acc_now[way, sl, :] = flash(s, m_now[way, sl, :], acc_now[way, sl, :], vext[way, at, :])

            @pl.when(j == KEY_BLOCKS // 2 - 1)
            def _():
                tick(2 * k + 2)

            @pl.when(j == KEY_BLOCKS - 1)
            def _():
                tick(2 * k + 3)
            return 0

        lax.fori_loop(0, KEY_BLOCKS, keys, 0)
        for t, way, other, off in places():
            at = pl.ds(off, n_rows)
            here = pl.ds(t * two + other * n_rows, n_rows)
            m_abs[way, at, :] = m_now[way, here, :]
            acc_abs[way, at, :] = acc_now[way, here, :]
        return 0

    lax.fori_loop(0, nz // 2, two_steps, 0)

    pieces = [(s, way) for s in range(1, nz // 2 + 1) for way in range(2) if s <= reach[way]]
    for s, way in pieces:
        for k in range(1, n_dp):
            b_copy(s, way, k, lax.rem(group + n_dp - k, n_dp)).wait_recv()
        c_copy(s, way).start()

    mine = pl.ds(pl.multiple_of(me * d, d), d)

    def o_copy(i, to):
        home = lax.rem(chip + 1 + i, nz)
        off = pl.multiple_of(home * two + to * n_rows, n_rows)
        return remote(o_v.at[:, pl.ds(off, n_rows), :], o_all.at[:, :, mine], o_send.at[i, to], o_recv.at[i, core], home * 2 + to)

    def own_chunk(i, _):
        home = lax.rem(chip + 1 + i, nz)
        at = pl.ds(pl.multiple_of(home * two, two), two)
        for way in range(2):
            s = lax.dot_general(q_abs[way, at, :], kn_ref[way], nt, preferred_element_type=f32)
            rid = lax.broadcasted_iota(jnp.int32, (two, 1), 0) + home * two
            s = jnp.where(lax.broadcasted_iota(jnp.int32, s.shape, 1) <= jnp.minimum(rid, c_ref[way] - 1), s, NEG)
            m_prev = jnp.where(jnp.full((two, d), p_ref[way], jnp.int32) > 0, m_abs[way, at, :], NEG)
            _, acc = flash(s, m_prev, acc_abs[way, at, :], vn_ext[way])
            o_v[way, at, :] = (acc[:, :d] / acc[:, d:]).astype(bf)
        for to in range(2):
            @pl.when((i < nz - 1) | (core != to))
            def _():
                o_copy(i, to).start()

            @pl.when((i == nz - 1) & (core == to))
            def _():
                o_all[:, :, mine] = o_v[:, pl.ds(pl.multiple_of(home * two + to * n_rows, n_rows), n_rows), :]
        return 0

    lax.fori_loop(0, nz, own_chunk, 0)

    def o_wait(i, _):
        for to in range(2):
            @pl.when((i < nz - 1) | (core != to))
            def _():
                source = lax.rem(chip + 2 * nz - 1 - i, nz) * 2 + to
                spot = pl.ds(pl.multiple_of(source * d, d), d)
                remote(o_v.at[:, pl.ds(0, n_rows), :], o_all.at[:, :, spot], o_send.at[i, to], o_recv.at[i, to], pair).wait_recv()
                o_copy(i, to).wait_send()
        return 0

    lax.fori_loop(0, nz, o_wait, 0)

    own_store.wait()
    c_copy(0, 0, wo).wait_send()
    c_wait(0, 0)
    for way in range(2):
        a_copy(0, way, own_share).wait_send()
    for s, way in pieces:
        c_wait(s, way)
        c_copy(s, way).wait_send()
        for k in range(1, n_dp):
            b_copy(s, way, k).wait_send()
        if s < reach[way]:
            a_copy(s, way).wait_send()
    for s in range(nz):
        for way in range(2):
            pair_copy(s, way).wait_send()
            if s < nz - 1:
                for h in range(CHUNKS):
                    ring_copy(s, way, h).wait_send()


def front(n_tp, n_dp, x, gain, prefix, valid, freq, bias, w_q, w_k, w_v, w_o, k_cache, v_cache):
    n_req, n_rows, width = x.shape
    d = w_q.shape[1]
    nz = n_tp // 2
    n_tok = n_rows * n_tp
    slots = k_cache.shape[1]
    old = slots - n_tok
    bf, f32 = jnp.bfloat16, jnp.float32
    any_spec = pl.BlockSpec(memory_space=pl.ANY)
    sm = pl.BlockSpec(memory_space=pltpu.SMEM)
    vm = pl.BlockSpec(memory_space=pltpu.VMEM)
    dma = pltpu.SemaphoreType.DMA
    made = jax.ShapeDtypeStruct((n_req, n_tok, d), bf)
    cache = jax.ShapeDtypeStruct(k_cache.shape, bf)
    return pl.pallas_call(
        functools.partial(front_kernel, n_tp, n_dp),
        out_shape=[jax.ShapeDtypeStruct(x.shape, bf), made, made, jax.ShapeDtypeStruct((n_tp * d, width), bf), cache, cache],
        in_specs=[sm, sm, vm, vm, vm, vm] + [any_spec] * 6,
        out_specs=[vm, vm, vm, any_spec, any_spec, any_spec],
        scratch_shapes=[
            pltpu.VMEM((width, 3 * d), bf),
            pltpu.VMEM((nz, 2, 2, n_rows, width), bf),
            pltpu.VMEM(w_o.shape, bf),
            pltpu.VMEM(k_cache.shape, bf),
            pltpu.VMEM(k_cache.shape, bf),
            pltpu.VMEM((n_req, old, 2 * d), bf),
            pltpu.VMEM((n_req, n_tok, d), bf),
            pltpu.VMEM((n_req, n_tok, 2 * d), bf),
            pltpu.VMEM((n_req, n_tok, d), f32),
            pltpu.VMEM((n_req, n_tok, 2 * d), f32),
            pltpu.VMEM((n_req, 4 * n_rows, d), bf),
            pltpu.VMEM((n_req, 4 * n_rows, d), f32),
            pltpu.VMEM((n_req, 4 * n_rows, 2 * d), f32),
            pltpu.VMEM((n_req, n_tok, d), bf),
            dma((4,)), dma((4,)), dma((nz, 2, CHUNKS)), dma((nz, 2, CHUNKS)), dma((nz, 2)), dma((nz, 2)),
            dma((nz, 2)), dma((nz, 2)), dma((nz, 2, n_dp)), dma((nz, 2, n_dp)), dma((nz, 2)), dma((nz, 2)),
            dma((nz, 2)), dma((nz, 2)),
        ],
        compiler_params=pltpu.CompilerParams(vmem_limit_bytes=62 * 2**20, collective_id=2, has_side_effects=True),
        cost_estimate=pl.CostEstimate(flops=8 * n_req * n_tok * slots * d, bytes_accessed=20 * 2**20, transcendentals=n_req * n_tok * slots),
        name="front",
    )(prefix, valid, x, gain.reshape(1, width), freq, bias, w_q, w_k, w_v, w_o, k_cache, v_cache)


def patch_kernel(p_ref, c_ref, kn_ref, vn_ref, ki_hbm, vi_hbm, ko_hbm, vo_hbm, window, shift, sems):
    n_req, n_tok, d = kn_ref.shape
    slots = ko_hbm.shape[1]
    win = window.shape[2]
    starts, moves_in, moves_out = [], [], []
    for r in range(n_req):
        start = pl.multiple_of(jnp.minimum((p_ref[r] // 16) * 16, slots - win), 16)
        starts.append(start)
        for i, (src, dst) in enumerate(((ki_hbm, ko_hbm), (vi_hbm, vo_hbm))):
            at = pl.ds(start, win)
            moves_in.append(pltpu.make_async_copy(src.at[r, at], window.at[r, i], sems.at[0, r, i]))
            moves_out.append(pltpu.make_async_copy(window.at[r, i], dst.at[r, at], sems.at[1, r, i]))
    for c in moves_in:
        c.start()
    for r in range(n_req):
        off = p_ref[r] - starts[r]
        at = lax.broadcasted_iota(jnp.int32, (win, d), 0) - off
        fresh = (at >= 0) & (at < c_ref[r])
        for i, new_ref in enumerate((kn_ref, vn_ref)):
            shift[pl.ds(16, n_tok), :] = new_ref[r].astype(jnp.float32)
            moved = shift[pl.ds(16 - off, win), :]
            moves_in[r * 2 + i].wait()
            window[r, i] = jnp.where(fresh, moved, window[r, i].astype(jnp.float32)).astype(window.dtype)
            moves_out[r * 2 + i].start()
    for c in moves_out:
        c.wait()


def patch(prefix, valid, k_new, v_new, k_all, v_all):
    n_req, n_tok, d = k_new.shape
    any_spec = pl.BlockSpec(memory_space=pl.ANY)
    sm = pl.BlockSpec(memory_space=pltpu.SMEM)
    vm = pl.BlockSpec(memory_space=pltpu.VMEM)
    same = jax.ShapeDtypeStruct(k_all.shape, k_all.dtype)
    return pl.pallas_call(
        patch_kernel,
        out_shape=[same, same],
        in_specs=[sm, sm, vm, vm, any_spec, any_spec],
        out_specs=[any_spec, any_spec],
        scratch_shapes=[
            pltpu.VMEM((n_req, 2, n_tok + 16, d), k_all.dtype),
            pltpu.VMEM((n_tok + 32, d), jnp.float32),
            pltpu.SemaphoreType.DMA((2, n_req, 2)),
        ],
        input_output_aliases={4: 0, 5: 1},
        compiler_params=pltpu.CompilerParams(vmem_limit_bytes=62 * 2**20),
        cost_estimate=pl.CostEstimate(flops=10**6, bytes_accessed=4 * 2**20, transcendentals=0),
        name="patch",
    )(prefix, valid, k_new, v_new, k_all, v_all)


def solution(mesh):
    n_tp = mesh.shape["tp"]
    row_spec = P("dp", "tp", None)
    cache_spec = P("dp", None, "tp", None)
    req_spec = P("dp")
    rep_spec = P(None)
    col_spec = P(None, "tp")
    bias_spec = P("tp")
    down_spec = P("tp", None)

    def layer(x_rows, k_cache, v_cache, prefix, valid, g_attn, w_q, b_q, w_k, b_k, w_v, b_v, w_o, g_mlp, w_gate, w_up, w_down):
        n_req, head_dim = x_rows.shape[0], k_cache.shape[-1]
        half = jnp.arange(head_dim // 2, dtype=jnp.float32)
        freq = ROPE_THETA ** (-(half * 2.0) / head_dim)
        freq = jnp.concatenate([freq, freq])[None]
        bias = jnp.concatenate([b_q, b_k, b_v])[None]
        flat = (n_req, -1, head_dim)
        o, k_new, v_new, w_o_full, k_all, v_all = front(n_tp, mesh.shape["dp"], x_rows, g_attn, prefix, valid, freq, bias, w_q, w_k, w_v, w_o, k_cache.reshape(flat), v_cache.reshape(flat))
        k_out, v_out = patch(prefix, valid, k_new, v_new, k_all, v_all)
        out = tail(n_tp, o, x_rows, g_mlp, w_o_full, w_gate.T, w_up.T, w_down)
        return out, k_out.reshape(k_cache.shape), v_out.reshape(v_cache.shape)

    in_specs = (row_spec, cache_spec, cache_spec, req_spec, req_spec, rep_spec, col_spec, bias_spec, col_spec, bias_spec, col_spec, bias_spec, down_spec, rep_spec, col_spec, col_spec, down_spec)
    return jax.shard_map(layer, mesh=mesh, in_specs=in_specs, out_specs=(row_spec, cache_spec, cache_spec), check_vma=False)
```

time: 231 us -> 213 us (0.922); the launches traced: 228 us -> 213 us
  Pallas kernels: 212 us -> 200 us
  local copies, waits for them, and re-layouts: 14.7 us -> 10.6 us
    pallas_call x1, Pallas kernels: 108 us -> 97.1 us  [tail(): pl.pallas_call(functools.partial(tail_kernel, n_tp), out_shape=jax.ShapeD...]
    unnamed x23 -> x7, local copies, waits for them, and re-layouts: 13.4 us -> 7.44 us
where the time goes in v4:
time: 213 us
  Pallas kernels  200 us (94%)
  local copies, waits for them, and re-layouts  10.6 us (5%)
    pallas_call x1, Pallas kernels, front(): pl.pallas_call(functools.partial(front_kernel, n_tp, n_dp), out_shape=[ja...  99.7 us
    pallas_call x1, Pallas kernels, tail(): pl.pallas_call(functools.partial(tail_kernel, n_tp), out_shape=jax.ShapeD...  97.1 us
    unnamed x7, local copies, waits for them, and re-layouts  7.44 us

profile of v4, /device:TPU:28, one launch (start us, length us, event | category | flops | bytes accessed | tf_op | source)
XLA Modules:
  0.0 213.0 jit_solution(5050033675154496177)
XLA Ops:
  0.6 0.7 maximum_bitcast_fusion.f_ref
  1.3 0.7 pad_maximum_fusion
  2.0 0.6 broadcast_in_dim.7.b_ref
  2.6 1.3 reshape.24.g_ref
  3.9 1.3 reshape.27.g_ref
  5.1 99.7 %front.1 = (bf16[2,64,2048]{2,1,0:T(8,128)(2,1)}, bf16[2,1024,128]{2,1,0:T(8,128)(2,1)}, bf16[2,1024,128]{2,1,0:T(8,128)(2,1)}, bf16[2048,2048]{1,0:T(8,128)(2,1...) custom-call(s32[2]{0:T(128)} %p_ref.3, s32[2]{0:T(128)} %c_ref.3, bf16[2,64,2048]{2,1,0:T(8,128)(2,1)} %x_ref.3, ...), custom_call_target="tpu_custom_call" | custom-call | flops 17179869184 | bytes 20971520 | tf_op jit(solution)/shard_map/front/pallas_call | solution.py:468
  104.9 97.1 %tail.1 = bf16[2,64,2048]{2,1,0:T(8,128)(2,1)} custom-call(bf16[2,64,2048]{2,1,0:T(8,128)(2,1)} %get-tuple-element.11.o_all, bf16[2,64,2048]{2,1,0:T(8,128)(2,1)} %x_ref.3, bf16[1,2048]{1,0:T(2,128)(2,1)} %reshape.27.g_ref, bf16[2048,2048]{1,0:T(8,128)(2,1)} %get-tuple-element.12.wo_hbm, bf16[688,2048]{1,0:T(8,128)(2,1)} %bitcast.16, ...), custom_call_target="tpu_custom_call" | custom-call | flops 17314086912 | bytes 20971520 | tf_op jit(solution)/shard_map/tail/pallas_call | solution.py:145
  201.9 0.0 copy-start.1
  202.0 3.6 %patch.1 = (bf16[2,8192,128]{2,1,0:T(8,128)(2,1)}, bf16[2,8192,128]{2,1,0:T(8,128)(2,1)}) custom-call(s32[2]{0:T(128)} %p_ref.3, s32[2]{0:T(128)} %c_ref.3, bf16[2,1024,128]{2,1,0:T(8,128)(2,1)} %get-tuple-element.13.kn_ref, bf16[2,1024,128]{2,1,0:T(8,128)(2,1)} %get-tuple-element.14.vn_ref, ...), custom_call_target="tpu_custom_call", output_to_operand_aliasing={{0}: (4, {}), {1}: (5, {})} | custom-call | flops 1000000 | bytes 4194304 | tf_op jit(solution)/shard_map/patch/pallas_call | solution.py:532
  205.6 0.0 copy-done.1
  205.6 0.8 copy.29
  206.4 0.0 copy-start
  206.4 4.6 %copy.30 = bf16[2,8192,1,128]{3,1,2,0:T(8,128)(2,1)} copy(bf16[2,8192,1,128]{3,1,2,0:T(8,128)(2,1)} %bitcast.12) | data formatting | bytes 8388608
  211.0 0.0 copy-done
  211.0 2.0 copy.31
  (1 shorter events, 0.0 us)
Async XLA Ops:
  201.9 3.7 %copy-start.1 = (bf16[2,64,2048]{2,1,0:T(8,128)(2,1)S(1)}, bf16[2,64,2048]{2,1,0:T(8,128)(2,1)}, u32[]{:S(2)}) copy-start(bf16[2,64,2048]{2,1,0:T(8,128)(2,1)} %tail.1) | copy-start | bytes 1572868
  206.4 4.6 %copy-start = (bf16[2,8192,128]{2,1,0:T(8,128)(2,1)S(1)}, bf16[2,8192,128]{2,1,0:T(8,128)(2,1)}, u32[]{:S(2)}) copy-start(bf16[2,8192,128]{2,1,0:T(8,128)(2,1)} %get-tuple-element.18) | copy-start | bytes 12582916

commit v5 on v4

--- a/solution.py
+++ b/solution.py
@@ -3,6 +3,7 @@
 
 import jax
 import jax.numpy as jnp
+import numpy as np
 from jax import lax
 from jax.experimental import pallas as pl
 from jax.experimental.pallas import tpu as pltpu
@@ -34,20 +35,21 @@
     n_req, n_rows, width = x_ref.shape
 
     loads = [pltpu.make_async_copy(s, t, load_sem.at[i]) for i, (s, t) in enumerate(((wo_hbm, wo), (wg_hbm, wg), (wu_hbm, wu), (wd_hbm, wd)))]
-    for c in loads:
-        c.start()
+    loads[0].start()
 
     barrier = pltpu.get_barrier_semaphore()
     for there in (up, down, pair):
         pl.semaphore_signal(barrier, inc=1, device_id={"tp": there}, device_id_type=MESH)
 
     loads[0].wait()
+    for c in loads[1:]:
+        c.start()
     mixed = jnp.dot(o_all[...].reshape(n_req * n_rows, width), wo[...], preferred_element_type=jnp.float32).astype(jnp.bfloat16)
     resid = (x_ref[...].reshape(n_req * n_rows, width).astype(jnp.float32) + mixed.astype(jnp.float32)).astype(jnp.bfloat16)
     x1[...] = resid.reshape(x1.shape)
     wide = resid.astype(jnp.float32)
     inv = lax.rsqrt(jnp.mean(wide * wide, axis=-1, keepdims=True) + NORM_EPS)
-    normed = (wide * inv * g_ref[...].astype(jnp.float32)).astype(jnp.bfloat16)
+    normed = (wide * inv * g_ref[...].astype(jnp.float32).reshape(1, width)).astype(jnp.bfloat16)
     pl.semaphore_wait(barrier, 3)
     rows[0, :, 0] = normed.reshape(n_req, n_rows, width)
 
@@ -166,15 +168,15 @@
         compiler_params=pltpu.CompilerParams(vmem_limit_bytes=62 * 2**20, collective_id=1, has_side_effects=True),
         cost_estimate=pl.CostEstimate(flops=6 * n_tp * n_req * n_rows * width * ffn, bytes_accessed=20 * 2**20, transcendentals=0),
         name="tail",
-    )(o, x, gain.reshape(1, width), w_o, w_gate, w_up, w_down)
+    )(o, x, gain, w_o, w_gate, w_up, w_down)
 
 
 NEG = -1.0e30
 KEY_BLOCKS = 4
 
 
-def front_kernel(n_tp, n_dp, p_ref, c_ref, x_ref, g_ref, f_ref, b_ref, wq_hbm, wk_hbm, wv_hbm, wo_hbm, kc_hbm, vc_hbm,
-                 o_all, kn_ref, vn_ref, all_hbm, ko_hbm, vo_hbm,
+def front_kernel(n_tp, n_dp, p_ref, c_ref, x_ref, g_ref, f_ref, bq_ref, bk_ref, bv_ref, wq_hbm, wk_hbm, wv_hbm, wo_hbm, kc_hbm, vc_hbm,
+                 o_all, kn_ref, vn_ref, all_hbm,
                  w, rows, wo, kc, vc, vext, q_abs, vn_ext, m_abs, acc_abs, q_now, m_now, acc_now, o_v,
                  load_sem, cache_sem, ring_send, ring_recv, pair_send, pair_recv, a_send, a_recv, b_send, b_recv, c_send, c_recv, o_send, o_recv):
     nz = n_tp // 2
@@ -197,8 +199,7 @@
     loads = [pltpu.make_async_copy(s, w.at[:, pl.ds(i * d, d)], load_sem.at[i]) for i, s in enumerate((wq_hbm, wk_hbm, wv_hbm))]
     for c in loads:
         c.start()
-    cache_in = [pltpu.make_async_copy(kc_hbm, kc, cache_sem.at[0]), pltpu.make_async_copy(vc_hbm, vc, cache_sem.at[1])]
-    cache_out = [pltpu.make_async_copy(kc, ko_hbm, cache_sem.at[2]), pltpu.make_async_copy(vc, vo_hbm, cache_sem.at[3])]
+    cache_in = [pltpu.make_async_copy(s.at[:, pl.ds(0, old)], t, cache_sem.at[i]) for i, (s, t) in enumerate(((kc_hbm, kc), (vc_hbm, vc)))]
     for c in cache_in:
         c.start()
 
@@ -210,7 +211,7 @@
 
     wide = x_ref[...].astype(f32)
     inv = lax.rsqrt(jnp.mean(wide * wide, axis=-1, keepdims=True) + NORM_EPS)
-    rows[0, :, 0] = (wide * inv * g_ref[...].astype(f32)).astype(bf)
+    rows[0, :, 0] = (wide * inv * g_ref[...].astype(f32).reshape(1, width)).astype(bf)
     pl.semaphore_wait(barrier, n_tp + n_dp - 2)
 
     span = n_rows // CHUNKS
@@ -262,10 +263,7 @@
     own_store.start()
     c_copy(0, 0, wo).start()
 
-    for i in range(2):
-        cache_in[i].wait()
-        cache_out[i].start()
-    for c in cache_out:
+    for c in cache_in:
         c.wait()
     tile = 1024
     for r in range(n_req):
@@ -320,40 +318,40 @@
 
     tick(1)
 
-    def two_steps(k, _):
+    def places(k):
+        for t in range(2):
+            for way in range(2):
+                for other in range(2):
+                    off = pl.multiple_of((away(2 * k + t, way) * 2 + (core if other == 0 else 1 - core)) * n_rows, n_rows)
+                    yield t, way, other, off
+
+    def project(k):
         for t in range(2):
             for way in range(2):
                 pair_copy(2 * k + t, way).wait_recv()
         lhs = rows[pl.ds(2 * k, 2)].reshape(8 * n_rows, width)
         total = jnp.dot(lhs, w[...], preferred_element_type=f32)
-        got = (total + b_ref[...].astype(f32)).astype(bf)
+        got = [(total[:, i * d:(i + 1) * d] + b[...].astype(f32).reshape(1, d)).astype(bf) for i, b in enumerate((bq_ref, bk_ref, bv_ref))]
         sign = jnp.where(lax.broadcasted_iota(jnp.int32, (n_rows, d), 1) < d // 2, -1.0, 1.0)
 
-        def places():
-            for t in range(2):
-                for way in range(2):
-                    for other in range(2):
-                        off = pl.multiple_of((away(2 * k + t, way) * 2 + (core if other == 0 else 1 - core)) * n_rows, n_rows)
-                        yield t, way, other, off
-
-        for t, way, other, off in places():
+        for t, way, other, off in places(k):
             at = pl.ds(off, n_rows)
             spot = (lax.broadcasted_iota(jnp.int32, (n_rows, d), 0) + (p_ref[way] + off)).astype(f32)
             angle = spot * f_ref[...]
             cos_t = jnp.cos(angle)
             sin_t = jnp.sin(angle) * sign
             i = ((t * 2 + way) * 2 + other) * n_rows
-            mine = got[i:i + n_rows]
             turned = []
-            for part in (mine[:, :d], mine[:, d:2 * d]):
-                part = part.astype(f32)
+            for part in got[:2]:
+                part = part[i:i + n_rows].astype(f32)
                 turned.append((part * cos_t + pltpu.roll(part, d // 2, 1) * sin_t).astype(bf))
             q_abs[way, at, :] = turned[0]
             q_now[way, pl.ds(t * two + other * n_rows, n_rows), :] = turned[0]
             kn_ref[way, at, :] = turned[1]
-            vn_ref[way, at, :] = mine[:, 2 * d:]
-            vn_ext[way, at, :d] = mine[:, 2 * d:]
-
+            vn_ref[way, at, :] = got[2][i:i + n_rows]
+            vn_ext[way, at, :d] = got[2][i:i + n_rows]
+
+    def attend_old(k, ticks):
         m_now[...] = jnp.full_like(m_now, NEG)
         acc_now[...] = jnp.zeros_like(acc_now)
 
@@ -365,24 +363,31 @@
                     s = lax.dot_general(q_now[way, sl, :], kc[way, at, :], nt, preferred_element_type=f32)
                     m_now[way, sl, :], acc_now[way, sl, :] = flash(s, m_now[way, sl, :], acc_now[way, sl, :], vext[way, at, :])
 
-            @pl.when(j == KEY_BLOCKS // 2 - 1)
-            def _():
-                tick(2 * k + 2)
-
-            @pl.when(j == KEY_BLOCKS - 1)
-            def _():
-                tick(2 * k + 3)
+            if ticks:
+                @pl.when(j == KEY_BLOCKS // 2 - 1)
+                def _():
+                    tick(2 * k + 2)
+
+                @pl.when(j == KEY_BLOCKS - 1)
+                def _():
+                    tick(2 * k + 3)
             return 0
 
         lax.fori_loop(0, KEY_BLOCKS, keys, 0)
-        for t, way, other, off in places():
+        for t, way, other, off in places(k):
             at = pl.ds(off, n_rows)
             here = pl.ds(t * two + other * n_rows, n_rows)
             m_abs[way, at, :] = m_now[way, here, :]
             acc_abs[way, at, :] = acc_now[way, here, :]
+
+    def two_steps(k, _):
+        project(k)
+        attend_old(k, True)
         return 0
 
-    lax.fori_loop(0, nz // 2, two_steps, 0)
+    last = nz // 2 - 1
+    lax.fori_loop(0, last, two_steps, 0)
+    project(last)
 
     pieces = [(s, way) for s in range(1, nz // 2 + 1) for way in range(2) if s <= reach[way]]
     for s, way in pieces:
@@ -392,41 +397,45 @@
 
     mine = pl.ds(pl.multiple_of(me * d, d), d)
 
-    def o_copy(i, to):
-        home = lax.rem(chip + 1 + i, nz)
+    def o_copy(s, way, to):
+        home = away(s, way)
         off = pl.multiple_of(home * two + to * n_rows, n_rows)
-        return remote(o_v.at[:, pl.ds(off, n_rows), :], o_all.at[:, :, mine], o_send.at[i, to], o_recv.at[i, core], home * 2 + to)
-
-    def own_chunk(i, _):
-        home = lax.rem(chip + 1 + i, nz)
-        at = pl.ds(pl.multiple_of(home * two, two), two)
-        for way in range(2):
+        return remote(o_v.at[way, pl.ds(off, n_rows), :], o_all.at[way, :, mine], o_send.at[s, way, to], o_recv.at[s, way, core], home * 2 + to)
+
+    def finish(i, _):
+        for way in range(2):
+            home = away(i, way)
+            at = pl.ds(pl.multiple_of(home * two, two), two)
             s = lax.dot_general(q_abs[way, at, :], kn_ref[way], nt, preferred_element_type=f32)
             rid = lax.broadcasted_iota(jnp.int32, (two, 1), 0) + home * two
             s = jnp.where(lax.broadcasted_iota(jnp.int32, s.shape, 1) <= jnp.minimum(rid, c_ref[way] - 1), s, NEG)
             m_prev = jnp.where(jnp.full((two, d), p_ref[way], jnp.int32) > 0, m_abs[way, at, :], NEG)
             _, acc = flash(s, m_prev, acc_abs[way, at, :], vn_ext[way])
             o_v[way, at, :] = (acc[:, :d] / acc[:, d:]).astype(bf)
-        for to in range(2):
-            @pl.when((i < nz - 1) | (core != to))
-            def _():
-                o_copy(i, to).start()
-
-            @pl.when((i == nz - 1) & (core == to))
-            def _():
-                o_all[:, :, mine] = o_v[:, pl.ds(pl.multiple_of(home * two + to * n_rows, n_rows), n_rows), :]
+        for way in range(2):
+            for to in range(2):
+                @pl.when((i > 0) | (core != to))
+                def _():
+                    o_copy(i, way, to).start()
+
+                @pl.when((i == 0) & (core == to))
+                def _():
+                    o_all[way, :, mine] = o_v[way, pl.ds(pl.multiple_of(chip * two + to * n_rows, n_rows), n_rows), :]
         return 0
 
-    lax.fori_loop(0, nz, own_chunk, 0)
+    lax.fori_loop(0, 2 * last, finish, 0)
+    attend_old(last, False)
+    lax.fori_loop(2 * last, nz, finish, 0)
 
     def o_wait(i, _):
-        for to in range(2):
-            @pl.when((i < nz - 1) | (core != to))
-            def _():
-                source = lax.rem(chip + 2 * nz - 1 - i, nz) * 2 + to
-                spot = pl.ds(pl.multiple_of(source * d, d), d)
-                remote(o_v.at[:, pl.ds(0, n_rows), :], o_all.at[:, :, spot], o_send.at[i, to], o_recv.at[i, to], pair).wait_recv()
-                o_copy(i, to).wait_send()
+        for way in range(2):
+            for to in range(2):
+                @pl.when((i > 0) | (core != to))
+                def _():
+                    source = away(i, 1 - way) * 2 + to
+                    spot = pl.ds(pl.multiple_of(source * d, d), d)
+                    remote(o_v.at[way, pl.ds(0, n_rows), :], o_all.at[way, :, spot], o_send.at[i, way, to], o_recv.at[i, way, to], pair).wait_recv()
+                    o_copy(i, way, to).wait_send()
         return 0
 
     lax.fori_loop(0, nz, o_wait, 0)
@@ -451,7 +460,7 @@
                     ring_copy(s, way, h).wait_send()
 
 
-def front(n_tp, n_dp, x, gain, prefix, valid, freq, bias, w_q, w_k, w_v, w_o, k_cache, v_cache):
+def front(n_tp, n_dp, x, gain, prefix, valid, freq, b_q, b_k, b_v, w_q, w_k, w_v, w_o, k_cache, v_cache):
     n_req, n_rows, width = x.shape
     d = w_q.shape[1]
     nz = n_tp // 2
@@ -464,18 +473,17 @@
     vm = pl.BlockSpec(memory_space=pltpu.VMEM)
     dma = pltpu.SemaphoreType.DMA
     made = jax.ShapeDtypeStruct((n_req, n_tok, d), bf)
-    cache = jax.ShapeDtypeStruct(k_cache.shape, bf)
     return pl.pallas_call(
         functools.partial(front_kernel, n_tp, n_dp),
-        out_shape=[jax.ShapeDtypeStruct(x.shape, bf), made, made, jax.ShapeDtypeStruct((n_tp * d, width), bf), cache, cache],
-        in_specs=[sm, sm, vm, vm, vm, vm] + [any_spec] * 6,
-        out_specs=[vm, vm, vm, any_spec, any_spec, any_spec],
+        out_shape=[jax.ShapeDtypeStruct(x.shape, bf), made, made, jax.ShapeDtypeStruct((n_tp * d, width), bf)],
+        in_specs=[sm, sm, vm, vm, vm, vm, vm, vm] + [any_spec] * 6,
+        out_specs=[vm, vm, vm, any_spec],
         scratch_shapes=[
             pltpu.VMEM((width, 3 * d), bf),
             pltpu.VMEM((nz, 2, 2, n_rows, width), bf),
             pltpu.VMEM(w_o.shape, bf),
-            pltpu.VMEM(k_cache.shape, bf),
-            pltpu.VMEM(k_cache.shape, bf),
+            pltpu.VMEM((n_req, old, d), bf),
+            pltpu.VMEM((n_req, old, d), bf),
             pltpu.VMEM((n_req, old, 2 * d), bf),
             pltpu.VMEM((n_req, n_tok, d), bf),
             pltpu.VMEM((n_req, n_tok, 2 * d), bf),
@@ -485,65 +493,62 @@
             pltpu.VMEM((n_req, 4 * n_rows, d), f32),
             pltpu.VMEM((n_req, 4 * n_rows, 2 * d), f32),
             pltpu.VMEM((n_req, n_tok, d), bf),
-            dma((4,)), dma((4,)), dma((nz, 2, CHUNKS)), dma((nz, 2, CHUNKS)), dma((nz, 2)), dma((nz, 2)),
+            dma((4,)), dma((2,)), dma((nz, 2, CHUNKS)), dma((nz, 2, CHUNKS)), dma((nz, 2)), dma((nz, 2)),
             dma((nz, 2)), dma((nz, 2)), dma((nz, 2, n_dp)), dma((nz, 2, n_dp)), dma((nz, 2)), dma((nz, 2)),
-            dma((nz, 2)), dma((nz, 2)),
+            dma((nz, 2, 2)), dma((nz, 2, 2)),
         ],
         compiler_params=pltpu.CompilerParams(vmem_limit_bytes=62 * 2**20, collective_id=2, has_side_effects=True),
         cost_estimate=pl.CostEstimate(flops=8 * n_req * n_tok * slots * d, bytes_accessed=20 * 2**20, transcendentals=n_req * n_tok * slots),
         name="front",
-    )(prefix, valid, x, gain.reshape(1, width), freq, bias, w_q, w_k, w_v, w_o, k_cache, v_cache)
-
-
-def patch_kernel(p_ref, c_ref, kn_ref, vn_ref, ki_hbm, vi_hbm, ko_hbm, vo_hbm, window, shift, sems):
+    )(prefix, valid, x, gain, freq, b_q, b_k, b_v, w_q, w_k, w_v, w_o, k_cache, v_cache)
+
+
+def merge_kernel(p_ref, c_ref, kn_ref, vn_ref, kc_hbm, vc_hbm, ko_hbm, vo_hbm, cache, shift, sems):
     n_req, n_tok, d = kn_ref.shape
     slots = ko_hbm.shape[1]
-    win = window.shape[2]
-    starts, moves_in, moves_out = [], [], []
-    for r in range(n_req):
-        start = pl.multiple_of(jnp.minimum((p_ref[r] // 16) * 16, slots - win), 16)
-        starts.append(start)
-        for i, (src, dst) in enumerate(((ki_hbm, ko_hbm), (vi_hbm, vo_hbm))):
-            at = pl.ds(start, win)
-            moves_in.append(pltpu.make_async_copy(src.at[r, at], window.at[r, i], sems.at[0, r, i]))
-            moves_out.append(pltpu.make_async_copy(window.at[r, i], dst.at[r, at], sems.at[1, r, i]))
+    win = n_tok + 16
+    news, olds, outs = (kn_ref, vn_ref), (kc_hbm, vc_hbm), (ko_hbm, vo_hbm)
+    pairs = [(r, i) for r in range(n_req) for i in range(2)]
+    moves_in = [pltpu.make_async_copy(olds[i].at[r], cache.at[r, i], sems.at[0, r, i]) for r, i in pairs]
+    moves_out = [pltpu.make_async_copy(cache.at[r, i], outs[i].at[r], sems.at[1, r, i]) for r, i in pairs]
     for c in moves_in:
         c.start()
-    for r in range(n_req):
-        off = p_ref[r] - starts[r]
+    for n, (r, i) in enumerate(pairs):
+        start = pl.multiple_of(jnp.minimum((p_ref[r] // 16) * 16, slots - win), 16)
+        off = p_ref[r] - start
         at = lax.broadcasted_iota(jnp.int32, (win, d), 0) - off
         fresh = (at >= 0) & (at < c_ref[r])
-        for i, new_ref in enumerate((kn_ref, vn_ref)):
-            shift[pl.ds(16, n_tok), :] = new_ref[r].astype(jnp.float32)
-            moved = shift[pl.ds(16 - off, win), :]
-            moves_in[r * 2 + i].wait()
-            window[r, i] = jnp.where(fresh, moved, window[r, i].astype(jnp.float32)).astype(window.dtype)
-            moves_out[r * 2 + i].start()
+        shift[pl.ds(16, n_tok), :] = news[i][r].astype(jnp.float32)
+        moved = shift[pl.ds(16 - off, win), :]
+        moves_in[n].wait()
+        part = pl.ds(start, win)
+        cache[r, i, part, :] = jnp.where(fresh, moved, cache[r, i, part, :].astype(jnp.float32)).astype(cache.dtype)
+        moves_out[n].start()
     for c in moves_out:
         c.wait()
 
 
-def patch(prefix, valid, k_new, v_new, k_all, v_all):
+def merge(prefix, valid, k_new, v_new, k_cache, v_cache):
     n_req, n_tok, d = k_new.shape
+    slots = k_cache.shape[1]
     any_spec = pl.BlockSpec(memory_space=pl.ANY)
     sm = pl.BlockSpec(memory_space=pltpu.SMEM)
     vm = pl.BlockSpec(memory_space=pltpu.VMEM)
-    same = jax.ShapeDtypeStruct(k_all.shape, k_all.dtype)
+    same = jax.ShapeDtypeStruct(k_cache.shape, k_cache.dtype)
     return pl.pallas_call(
-        patch_kernel,
+        merge_kernel,
         out_shape=[same, same],
         in_specs=[sm, sm, vm, vm, any_spec, any_spec],
         out_specs=[any_spec, any_spec],
         scratch_shapes=[
-            pltpu.VMEM((n_req, 2, n_tok + 16, d), k_all.dtype),
+            pltpu.VMEM((n_req, 2, slots, d), k_cache.dtype),
             pltpu.VMEM((n_tok + 32, d), jnp.float32),
             pltpu.SemaphoreType.DMA((2, n_req, 2)),
         ],
-        input_output_aliases={4: 0, 5: 1},
         compiler_params=pltpu.CompilerParams(vmem_limit_bytes=62 * 2**20),
-        cost_estimate=pl.CostEstimate(flops=10**6, bytes_accessed=4 * 2**20, transcendentals=0),
-        name="patch",
-    )(prefix, valid, k_new, v_new, k_all, v_all)
+        cost_estimate=pl.CostEstimate(flops=10**6, bytes_accessed=16 * 2**20, transcendentals=0),
+        name="merge",
+    )(prefix, valid, k_new, v_new, k_cache, v_cache)
 
 
 def solution(mesh):
@@ -558,13 +563,13 @@
 
     def layer(x_rows, k_cache, v_cache, prefix, valid, g_attn, w_q, b_q, w_k, b_k, w_v, b_v, w_o, g_mlp, w_gate, w_up, w_down):
         n_req, head_dim = x_rows.shape[0], k_cache.shape[-1]
-        half = jnp.arange(head_dim // 2, dtype=jnp.float32)
-        freq = ROPE_THETA ** (-(half * 2.0) / head_dim)
-        freq = jnp.concatenate([freq, freq])[None]
-        bias = jnp.concatenate([b_q, b_k, b_v])[None]
+        half = np.arange(head_dim // 2, dtype=np.float32)
+        freq = np.float32(ROPE_THETA) ** (-(half * np.float32(2.0)) / np.float32(head_dim))
+        freq = jnp.asarray(np.concatenate([freq, freq])[None], jnp.float32)
         flat = (n_req, -1, head_dim)
-        o, k_new, v_new, w_o_full, k_all, v_all = front(n_tp, mesh.shape["dp"], x_rows, g_attn, prefix, valid, freq, bias, w_q, w_k, w_v, w_o, k_cache.reshape(flat), v_cache.reshape(flat))
-        k_out, v_out = patch(prefix, valid, k_new, v_new, k_all, v_all)
+        k_flat, v_flat = k_cache.reshape(flat), v_cache.reshape(flat)
+        o, k_new, v_new, w_o_full = front(n_tp, mesh.shape["dp"], x_rows, g_attn, prefix, valid, freq, b_q, b_k, b_v, w_q, w_k, w_v, w_o, k_flat, v_flat)
+        k_out, v_out = merge(prefix, valid, k_new, v_new, k_flat, v_flat)
         out = tail(n_tp, o, x_rows, g_mlp, w_o_full, w_gate.T, w_up.T, w_down)
         return out, k_out.reshape(k_cache.shape), v_out.reshape(v_cache.shape)
 

time: 213 us -> 203 us (0.953)
  local copies, waits for them, and re-layouts: 10.6 us -> 0.8 us
    unnamed x7 -> x3, local copies, waits for them, and re-layouts: 7.44 us -> 0.8 us
    pallas_call x1, Pallas kernels: 99.7 us -> 94.8 us  [front(): pl.pallas_call(functools.partial(front_kernel, n_tp, n_dp), out_shape=[ja...]
    pallas_call x1, Pallas kernels: 3.63 us -> 8.05 us  [merge(): pl.pallas_call(merge_kernel, out_shape=[same, same], in_specs=[sm, sm, vm...]
    reshape x2 -> x0, local copies, waits for them, and re-layouts: 2.58 us -> none  [the longest x1 1.29 us: front(): gain.reshape(1, width)]
where the time goes in v5:
time: 203 us; the launch traced here: 202 us
  Pallas kernels  201 us (99%)
    pallas_call x1, Pallas kernels, tail(): pl.pallas_call(functools.partial(tail_kernel, n_tp), out_shape=jax.ShapeD...  98 us
    pallas_call x1, Pallas kernels, front(): pl.pallas_call(functools.partial(front_kernel, n_tp, n_dp), out_shape=[ja...  94.8 us
    pallas_call x1, Pallas kernels, merge(): pl.pallas_call(merge_kernel, out_shape=[same, same], in_specs=[sm, sm, vm...  8.05 us

profile of v5, /device:TPU:28, one launch (start us, length us, event | category | flops | bytes accessed | tf_op | source)
XLA Modules:
  0.0 202.3 jit_solution(6988994901080844475)
XLA Ops:
  0.6 94.8 %front.1 = (bf16[2,64,2048]{2,1,0:T(8,128)(2,1)}, bf16[2,1024,128]{2,1,0:T(8,128)(2,1)}, bf16[2,1024,128]{2,1,0:T(8,128)(2,1)}, bf16[2048,2048]{1,0:T(8,128)(2,1)}) custom-call(s32[2]{0:T(128)} %p_ref.3, s32[2]{0:T(128)} %c_ref.3, bf16[2,64,2048]{2,1,0:T(8,128)(2,1)} %x_ref.3, bf16[2048]{0:T(1024)(128)(2,1)} %g_ref.2, f32[1,128]{1,0:T(1,128)} %constant.2.clone.f_ref, ...), custom_call_target="tpu_custom_call" | custom-call | flops 17179869184 | bytes 20971520 | tf_op jit(solution)/shard_map/front/pallas_call | solution.py:476
  95.4 98.0 %tail.1 = bf16[2,64,2048]{2,1,0:T(8,128)(2,1)} custom-call(bf16[2,64,2048]{2,1,0:T(8,128)(2,1)} %get-tuple-element.9.o_all, bf16[2,64,2048]{2,1,0:T(8,128)(2,1)} %x_ref.3, bf16[2048]{0:T(1024)(128)(2,1)} %g_ref.3, bf16[2048,2048]{1,0:T(8,128)(2,1)} %get-tuple-element.10.wo_hbm, bf16[688,2048]{1,0:T(8,128)(2,1)} %bitcast.16, bf16[688,2048]{1,0:T(8,128)(2,1)} %bitcast.17, ...), custom_call_target="tpu_custom_call" | custom-call | flops 17314086912 | bytes 20971520 | tf_op jit(solution)/shard_map/tail/pallas_call | solution.py:147
  193.4 0.0 copy-start
  193.4 8.1 %merge.1 = (bf16[2,8192,128]{2,1,0:T(8,128)(2,1)}, bf16[2,8192,128]{2,1,0:T(8,128)(2,1)}) custom-call(s32[2]{0:T(128)} %p_ref.3, s32[2]{0:T(128)} %c_ref.3, bf16[2,1024,128]{2,1,0:T(8,128)(2,1)} %get-tuple-element.11.kn_ref, bf16[2,1024,128]{2,1,0:T(8,128)(2,1)} %get-tuple-element.12.vn_ref, bf16[2,8192,128]{2,1,0:T(8,128)(2,1)} %bitcast.11, ...), custom_call_target="tpu_custom_call" | custom-call | flops 1000000 | bytes 16777216 | tf_op jit(solution)/shard_map/merge/pallas_call | solution.py:538
  201.5 0.0 copy-done
  201.5 0.8 copy.24
Async XLA Ops:
  193.4 8.1 %copy-start = (bf16[2,64,2048]{2,1,0:T(8,128)(2,1)S(1)}, bf16[2,64,2048]{2,1,0:T(8,128)(2,1)}, u32[]{:S(2)}) copy-start(bf16[2,64,2048]{2,1,0:T(8,128)(2,1)} %tail.1) | copy-start | bytes 1572868

commit v6 on v5

--- a/solution.py
+++ b/solution.py
@@ -13,7 +13,8 @@
 NORM_EPS = 1.0e-6
 
 
-CHUNKS = 2
+CHUNKS = 1
+WO_BITES = 4
 MESH = pl.DeviceIdType.MESH
 
 
@@ -23,7 +24,7 @@
 
 def tail_kernel(n_tp, o_all, x_ref, g_ref, wo_hbm, wg_hbm, wu_hbm, wd_hbm, out_ref,
                 wo, wg, wu, wd, x1, rows, sums_in, sums_out, part_in, part_out, kept,
-                load_sem, ring_send, ring_recv, pair_send, pair_recv, sum_send, sum_recv, part_send, part_recv):
+                load_sem, bite_sem, ring_send, ring_recv, pair_send, pair_recv, sum_send, sum_recv, part_send, part_recv):
     nz = n_tp // 2
     me = lax.axis_index("tp")
     core = lax.rem(me, 2)
@@ -34,17 +35,27 @@
     towards = (up, down)
     n_req, n_rows, width = x_ref.shape
 
-    loads = [pltpu.make_async_copy(s, t, load_sem.at[i]) for i, (s, t) in enumerate(((wo_hbm, wo), (wg_hbm, wg), (wu_hbm, wu), (wd_hbm, wd)))]
-    loads[0].start()
+    loads = [pltpu.make_async_copy(s, t, load_sem.at[i]) for i, (s, t) in enumerate(((wg_hbm, wg), (wu_hbm, wu), (wd_hbm, wd)))]
+    bite = wo.shape[0] // WO_BITES
+    bites = [pltpu.make_async_copy(wo_hbm.at[pl.ds(i * bite, bite)], wo.at[pl.ds(i * bite, bite)], bite_sem.at[i]) for i in range(WO_BITES)]
+    for c in bites:
+        c.start()
 
     barrier = pltpu.get_barrier_semaphore()
     for there in (up, down, pair):
         pl.semaphore_signal(barrier, inc=1, device_id={"tp": there}, device_id_type=MESH)
 
-    loads[0].wait()
-    for c in loads[1:]:
-        c.start()
-    mixed = jnp.dot(o_all[...].reshape(n_req * n_rows, width), wo[...], preferred_element_type=jnp.float32).astype(jnp.bfloat16)
+    heads = o_all[...].reshape(n_req * n_rows, width)
+    mixed = None
+    for i in range(WO_BITES):
+        bites[i].wait()
+        if i == WO_BITES - 1:
+            for c in loads:
+                c.start()
+        at = slice(i * bite, (i + 1) * bite)
+        piece = jnp.dot(heads[:, at], wo[at, :], preferred_element_type=jnp.float32)
+        mixed = piece if mixed is None else mixed + piece
+    mixed = mixed.astype(jnp.bfloat16)
     resid = (x_ref[...].reshape(n_req * n_rows, width).astype(jnp.float32) + mixed.astype(jnp.float32)).astype(jnp.bfloat16)
     x1[...] = resid.reshape(x1.shape)
     wide = resid.astype(jnp.float32)
@@ -53,8 +64,8 @@
     pl.semaphore_wait(barrier, 3)
     rows[0, :, 0] = normed.reshape(n_req, n_rows, width)
 
-    for i in (1, 2, 3):
-        loads[i].wait()
+    for c in loads:
+        c.wait()
 
     span = n_rows // CHUNKS
 
@@ -161,7 +172,7 @@
             pltpu.VMEM((nz, 2, n_rows, width), bf),
             pltpu.VMEM((nz, 2, n_rows, width), bf),
             pltpu.VMEM((2, 2, n_rows, width), jnp.float32),
-            dma((4,)),
+            dma((3,)), dma((WO_BITES,)),
             dma((nz, 2, CHUNKS)), dma((nz, 2, CHUNKS)), dma((nz, 2)), dma((nz, 2)),
             dma((nz, 2, CHUNKS)), dma((nz + 1, 2, CHUNKS)), dma((nz,)), dma((nz,)),
         ],
@@ -173,11 +184,12 @@
 
 NEG = -1.0e30
 KEY_BLOCKS = 4
+STREAMS = 2
 
 
 def front_kernel(n_tp, n_dp, p_ref, c_ref, x_ref, g_ref, f_ref, bq_ref, bk_ref, bv_ref, wq_hbm, wk_hbm, wv_hbm, wo_hbm, kc_hbm, vc_hbm,
                  o_all, kn_ref, vn_ref, all_hbm,
-                 w, rows, wo, kc, vc, vext, q_abs, vn_ext, m_abs, acc_abs, q_now, m_now, acc_now, o_v,
+                 w, rows, wo, cos_v, sin_v, kc, vc, vext, q_abs, vn_ext, m_abs, acc_abs, q_now, m_now, acc_now, o_v,
                  load_sem, cache_sem, ring_send, ring_recv, pair_send, pair_recv, a_send, a_recv, b_send, b_recv, c_send, c_recv, o_send, o_recv):
     nz = n_tp // 2
     me = lax.axis_index("tp")
@@ -214,10 +226,10 @@
     rows[0, :, 0] = (wide * inv * g_ref[...].astype(f32).reshape(1, width)).astype(bf)
     pl.semaphore_wait(barrier, n_tp + n_dp - 2)
 
-    span = n_rows // CHUNKS
+    span = n_rows // STREAMS
 
     def ring_copy(s, way, h):
-        part = pl.ds(h * span, span)
+        part = pl.ds(pl.multiple_of(h * span, span), span)
         return remote(rows.at[s, way, 0, part], rows.at[s + 1, way, 0, part], ring_send.at[s, way, h], ring_recv.at[s + 1, way, h], towards[way])
 
     def pair_copy(s, way):
@@ -250,7 +262,7 @@
         at = pl.ds(pl.multiple_of((away(s, way) * 2 + 1 - core) * n_own, 8), n_own)
         remote(all_hbm.at[at], all_hbm.at[at], c_send.at[s, way], c_recv.at[s, way], pair).wait_recv()
 
-    for h in range(CHUNKS):
+    for h in range(STREAMS):
         for way in range(2):
             ring_copy(0, way, h).start()
     for way in range(2):
@@ -277,21 +289,35 @@
             return 0
 
         lax.fori_loop(0, old // tile, tidy, 0)
+    turn = 128
+    sign = jnp.where(lax.broadcasted_iota(jnp.int32, (turn, d), 1) < d // 2, -1.0, 1.0)
+    for r in range(n_req):
+        def angles(t, _):
+            spot = (lax.broadcasted_iota(jnp.int32, (turn, d), 0) + (p_ref[r] + t * turn)).astype(f32)
+            angle = spot * f_ref[...]
+            at = pl.ds(pl.multiple_of(t * turn, turn), turn)
+            cos_v[r, at, :] = jnp.cos(angle)
+            sin_v[r, at, :] = jnp.sin(angle) * sign
+            return 0
+
+        lax.fori_loop(0, cos_v.shape[1] // turn, angles, 0)
     vn_ext[:, :, d:] = jnp.ones((n_req, vn_ext.shape[1], d), bf)
     for c in loads:
         c.wait()
 
-    def tick(s):
+    def pass_on(s, h):
         @pl.when(s < nz)
         def _():
-            for h in range(CHUNKS):
-                for way in range(2):
-                    ring_copy(s - 1, way, h).wait_recv()
-
-                    @pl.when(s < nz - 1)
-                    def _():
-                        ring_copy(s, way, h).start()
-
+            for way in range(2):
+                ring_copy(s - 1, way, h).wait_recv()
+
+                @pl.when(s < nz - 1)
+                def _():
+                    ring_copy(s, way, h).start()
+
+    def landed(s):
+        @pl.when(s < nz)
+        def _():
             for way in range(2):
                 pair_copy(s, way).start()
 
@@ -316,7 +342,9 @@
         p = jnp.exp2((s - m_new[:, :1]) * scale2).astype(bf)
         return m_new, acc * jnp.concatenate([a, a], axis=1) + jnp.dot(p, vals, preferred_element_type=f32)
 
-    tick(1)
+    for h in range(STREAMS):
+        pass_on(1, h)
+    landed(1)
 
     def places(k):
         for t in range(2):
@@ -332,14 +360,10 @@
         lhs = rows[pl.ds(2 * k, 2)].reshape(8 * n_rows, width)
         total = jnp.dot(lhs, w[...], preferred_element_type=f32)
         got = [(total[:, i * d:(i + 1) * d] + b[...].astype(f32).reshape(1, d)).astype(bf) for i, b in enumerate((bq_ref, bk_ref, bv_ref))]
-        sign = jnp.where(lax.broadcasted_iota(jnp.int32, (n_rows, d), 1) < d // 2, -1.0, 1.0)
 
         for t, way, other, off in places(k):
             at = pl.ds(off, n_rows)
-            spot = (lax.broadcasted_iota(jnp.int32, (n_rows, d), 0) + (p_ref[way] + off)).astype(f32)
-            angle = spot * f_ref[...]
-            cos_t = jnp.cos(angle)
-            sin_t = jnp.sin(angle) * sign
+            cos_t, sin_t = cos_v[way, at, :], sin_v[way, at, :]
             i = ((t * 2 + way) * 2 + other) * n_rows
             turned = []
             for part in got[:2]:
@@ -364,13 +388,14 @@
                     m_now[way, sl, :], acc_now[way, sl, :] = flash(s, m_now[way, sl, :], acc_now[way, sl, :], vext[way, at, :])
 
             if ticks:
-                @pl.when(j == KEY_BLOCKS // 2 - 1)
-                def _():
-                    tick(2 * k + 2)
-
-                @pl.when(j == KEY_BLOCKS - 1)
-                def _():
-                    tick(2 * k + 3)
+                for n in range(2 * STREAMS // KEY_BLOCKS):
+                    event = j * (2 * STREAMS // KEY_BLOCKS) + n
+                    step = 2 * k + 2 + event // STREAMS
+                    pass_on(step, lax.rem(event, STREAMS))
+
+                    @pl.when(lax.rem(event, STREAMS) == STREAMS - 1)
+                    def _():
+                        landed(step)
             return 0
 
         lax.fori_loop(0, KEY_BLOCKS, keys, 0)
@@ -456,7 +481,7 @@
         for way in range(2):
             pair_copy(s, way).wait_send()
             if s < nz - 1:
-                for h in range(CHUNKS):
+                for h in range(STREAMS):
                     ring_copy(s, way, h).wait_send()
 
 
@@ -482,6 +507,8 @@
             pltpu.VMEM((width, 3 * d), bf),
             pltpu.VMEM((nz, 2, 2, n_rows, width), bf),
             pltpu.VMEM(w_o.shape, bf),
+            pltpu.VMEM((n_req, n_tok, d), f32),
+            pltpu.VMEM((n_req, n_tok, d), f32),
             pltpu.VMEM((n_req, old, d), bf),
             pltpu.VMEM((n_req, old, d), bf),
             pltpu.VMEM((n_req, old, 2 * d), bf),
@@ -493,7 +520,7 @@
             pltpu.VMEM((n_req, 4 * n_rows, d), f32),
             pltpu.VMEM((n_req, 4 * n_rows, 2 * d), f32),
             pltpu.VMEM((n_req, n_tok, d), bf),
-            dma((4,)), dma((2,)), dma((nz, 2, CHUNKS)), dma((nz, 2, CHUNKS)), dma((nz, 2)), dma((nz, 2)),
+            dma((4,)), dma((2,)), dma((nz, 2, STREAMS)), dma((nz, 2, STREAMS)), dma((nz, 2)), dma((nz, 2)),
             dma((nz, 2)), dma((nz, 2)), dma((nz, 2, n_dp)), dma((nz, 2, n_dp)), dma((nz, 2)), dma((nz, 2)),
             dma((nz, 2, 2)), dma((nz, 2, 2)),
         ],
@@ -503,22 +530,25 @@
     )(prefix, valid, x, gain, freq, b_q, b_k, b_v, w_q, w_k, w_v, w_o, k_cache, v_cache)
 
 
-def merge_kernel(p_ref, c_ref, kn_ref, vn_ref, kc_hbm, vc_hbm, ko_hbm, vo_hbm, cache, shift, sems):
-    n_req, n_tok, d = kn_ref.shape
+def merge_kernel(p_ref, c_ref, kn_hbm, vn_hbm, kc_hbm, vc_hbm, ko_hbm, vo_hbm, cache, fresh_rows, shift, sems, new_sem):
+    n_req, n_tok, d = kn_hbm.shape
     slots = ko_hbm.shape[1]
     win = n_tok + 16
-    news, olds, outs = (kn_ref, vn_ref), (kc_hbm, vc_hbm), (ko_hbm, vo_hbm)
+    olds, outs = (kc_hbm, vc_hbm), (ko_hbm, vo_hbm)
+    new_in = [pltpu.make_async_copy(h, fresh_rows.at[i], new_sem.at[i]) for i, h in enumerate((kn_hbm, vn_hbm))]
     pairs = [(r, i) for r in range(n_req) for i in range(2)]
     moves_in = [pltpu.make_async_copy(olds[i].at[r], cache.at[r, i], sems.at[0, r, i]) for r, i in pairs]
     moves_out = [pltpu.make_async_copy(cache.at[r, i], outs[i].at[r], sems.at[1, r, i]) for r, i in pairs]
-    for c in moves_in:
+    for c in new_in + moves_in:
         c.start()
+    for c in new_in:
+        c.wait()
     for n, (r, i) in enumerate(pairs):
         start = pl.multiple_of(jnp.minimum((p_ref[r] // 16) * 16, slots - win), 16)
         off = p_ref[r] - start
         at = lax.broadcasted_iota(jnp.int32, (win, d), 0) - off
         fresh = (at >= 0) & (at < c_ref[r])
-        shift[pl.ds(16, n_tok), :] = news[i][r].astype(jnp.float32)
+        shift[pl.ds(16, n_tok), :] = fresh_rows[i, r].astype(jnp.float32)
         moved = shift[pl.ds(16 - off, win), :]
         moves_in[n].wait()
         part = pl.ds(start, win)
@@ -533,17 +563,18 @@
     slots = k_cache.shape[1]
     any_spec = pl.BlockSpec(memory_space=pl.ANY)
     sm = pl.BlockSpec(memory_space=pltpu.SMEM)
-    vm = pl.BlockSpec(memory_space=pltpu.VMEM)
     same = jax.ShapeDtypeStruct(k_cache.shape, k_cache.dtype)
     return pl.pallas_call(
         merge_kernel,
         out_shape=[same, same],
-        in_specs=[sm, sm, vm, vm, any_spec, any_spec],
+        in_specs=[sm, sm] + [any_spec] * 4,
         out_specs=[any_spec, any_spec],
         scratch_shapes=[
             pltpu.VMEM((n_req, 2, slots, d), k_cache.dtype),
+            pltpu.VMEM((2, n_req, n_tok, d), k_new.dtype),
             pltpu.VMEM((n_tok + 32, d), jnp.float32),
             pltpu.SemaphoreType.DMA((2, n_req, 2)),
+            pltpu.SemaphoreType.DMA((2,)),
         ],
         compiler_params=pltpu.CompilerParams(vmem_limit_bytes=62 * 2**20),
         cost_estimate=pl.CostEstimate(flops=10**6, bytes_accessed=16 * 2**20, transcendentals=0),

time: 203 us -> 195 us (0.961)
  Pallas kernels: 201 us -> 194 us
    pallas_call x1, Pallas kernels: 94.8 us -> 89.8 us  [front(): pl.pallas_call(functools.partial(front_kernel, n_tp, n_dp), out_shape=[ja...]
where the time goes in v6:
time: 195 us
  Pallas kernels  194 us (99%)
    pallas_call x1, Pallas kernels, tail(): pl.pallas_call(functools.partial(tail_kernel, n_tp), out_shape=jax.ShapeD...  96.2 us
    pallas_call x1, Pallas kernels, front(): pl.pallas_call(functools.partial(front_kernel, n_tp, n_dp), out_shape=[ja...  89.8 us
    pallas_call x1, Pallas kernels, merge(): pl.pallas_call(merge_kernel, out_shape=[same, same], in_specs=[sm, sm] +...  7.52 us

profile of v6, /device:TPU:28, one launch (start us, length us, event | category | flops | bytes accessed | tf_op | source)
XLA Modules:
  0.0 195.0 jit_solution(4727430709870957085)
XLA Ops:
  0.6 89.8 %front.1 = (bf16[2,64,2048]{2,1,0:T(8,128)(2,1)}, bf16[2,1024,128]{2,1,0:T(8,128)(2,1)}, bf16[2,1024,128]{2,1,0:T(8,128)(2,1)}, bf16[2048,2048]{1,0:T(8,128)(2,1)}) custom-call(s32[2]{0:T(128)} %p_ref.3, s32[2]{0:T(128)} %c_ref.3, bf16[2,64,2048]{2,1,0:T(8,128)(2,1)} %x_ref.3, bf16[2048]{0:T(1024)(128)(2,1)} %g_ref.2, f32[1,128]{1,0:T(1,128)} %constant.2.clone.f_ref, ...), custom_call_target="tpu_custom_call" | custom-call | flops 17179869184 | bytes 20971520 | tf_op jit(solution)/shard_map/front/pallas_call | solution.py:501
  90.4 96.2 %tail.1 = bf16[2,64,2048]{2,1,0:T(8,128)(2,1)} custom-call(bf16[2,64,2048]{2,1,0:T(8,128)(2,1)} %get-tuple-element.9.o_all, bf16[2,64,2048]{2,1,0:T(8,128)(2,1)} %x_ref.3, bf16[2048]{0:T(1024)(128)(2,1)} %g_ref.3, bf16[2048,2048]{1,0:T(8,128)(2,1)} %get-tuple-element.10.wo_hbm, bf16[688,2048]{1,0:T(8,128)(2,1)} %bitcast.16, bf16[688,2048]{1,0:T(8,128)(2,1)} %bitcast.17, ...), custom_call_target="tpu_custom_call" | custom-call | flops 17314086912 | bytes 20971520 | tf_op jit(solution)/shard_map/tail/pallas_call | solution.py:158
  186.6 0.0 copy-start
  186.6 7.5 %merge.1 = (bf16[2,8192,128]{2,1,0:T(8,128)(2,1)}, bf16[2,8192,128]{2,1,0:T(8,128)(2,1)}) custom-call(s32[2]{0:T(128)} %p_ref.3, s32[2]{0:T(128)} %c_ref.3, bf16[2,1024,128]{2,1,0:T(8,128)(2,1)} %get-tuple-element.11.kn_hbm, bf16[2,1024,128]{2,1,0:T(8,128)(2,1)} %get-tuple-element.12.vn_hbm, bf16[2,8192,128]{2,1,0:T(8,128)(2,1)} %bitcast.11, ...), custom_call_target="tpu_custom_call" | custom-call | flops 1000000 | bytes 16777216 | tf_op jit(solution)/shard_map/merge/pallas_call | solution.py:567
  194.2 0.0 copy-done
  194.2 0.8 copy.24
Async XLA Ops:
  186.6 7.5 %copy-start = (bf16[2,64,2048]{2,1,0:T(8,128)(2,1)S(1)}, bf16[2,64,2048]{2,1,0:T(8,128)(2,1)}, u32[]{:S(2)}) copy-start(bf16[2,64,2048]{2,1,0:T(8,128)(2,1)} %tail.1) | copy-start | bytes 1572868

commit v7 on v6

--- a/solution.py
+++ b/solution.py
@@ -530,7 +530,7 @@
     )(prefix, valid, x, gain, freq, b_q, b_k, b_v, w_q, w_k, w_v, w_o, k_cache, v_cache)
 
 
-def merge_kernel(p_ref, c_ref, kn_hbm, vn_hbm, kc_hbm, vc_hbm, ko_hbm, vo_hbm, cache, fresh_rows, shift, sems, new_sem):
+def merge_kernel(p_ref, c_ref, x_hbm, kn_hbm, vn_hbm, kc_hbm, vc_hbm, xo_hbm, ko_hbm, vo_hbm, x_v, cache, fresh_rows, shift, sems, new_sem, x_sem):
     n_req, n_tok, d = kn_hbm.shape
     slots = ko_hbm.shape[1]
     win = n_tok + 16
@@ -539,10 +539,14 @@
     pairs = [(r, i) for r in range(n_req) for i in range(2)]
     moves_in = [pltpu.make_async_copy(olds[i].at[r], cache.at[r, i], sems.at[0, r, i]) for r, i in pairs]
     moves_out = [pltpu.make_async_copy(cache.at[r, i], outs[i].at[r], sems.at[1, r, i]) for r, i in pairs]
-    for c in new_in + moves_in:
+    x_in = pltpu.make_async_copy(x_hbm, x_v, x_sem.at[0])
+    x_out = pltpu.make_async_copy(x_v, xo_hbm, x_sem.at[1])
+    for c in new_in + [x_in] + moves_in:
         c.start()
     for c in new_in:
         c.wait()
+    x_in.wait()
+    x_out.start()
     for n, (r, i) in enumerate(pairs):
         start = pl.multiple_of(jnp.minimum((p_ref[r] // 16) * 16, slots - win), 16)
         off = p_ref[r] - start
@@ -556,9 +560,10 @@
         moves_out[n].start()
     for c in moves_out:
         c.wait()
-
-
-def merge(prefix, valid, k_new, v_new, k_cache, v_cache):
+    x_out.wait()
+
+
+def merge(prefix, valid, x_new, k_new, v_new, k_cache, v_cache):
     n_req, n_tok, d = k_new.shape
     slots = k_cache.shape[1]
     any_spec = pl.BlockSpec(memory_space=pl.ANY)
@@ -566,20 +571,22 @@
     same = jax.ShapeDtypeStruct(k_cache.shape, k_cache.dtype)
     return pl.pallas_call(
         merge_kernel,
-        out_shape=[same, same],
-        in_specs=[sm, sm] + [any_spec] * 4,
-        out_specs=[any_spec, any_spec],
+        out_shape=[jax.ShapeDtypeStruct(x_new.shape, x_new.dtype), same, same],
+        in_specs=[sm, sm] + [any_spec] * 5,
+        out_specs=[any_spec] * 3,
         scratch_shapes=[
+            pltpu.VMEM(x_new.shape, x_new.dtype),
             pltpu.VMEM((n_req, 2, slots, d), k_cache.dtype),
             pltpu.VMEM((2, n_req, n_tok, d), k_new.dtype),
             pltpu.VMEM((n_tok + 32, d), jnp.float32),
             pltpu.SemaphoreType.DMA((2, n_req, 2)),
             pltpu.SemaphoreType.DMA((2,)),
+            pltpu.SemaphoreType.DMA((2,)),
         ],
         compiler_params=pltpu.CompilerParams(vmem_limit_bytes=62 * 2**20),
         cost_estimate=pl.CostEstimate(flops=10**6, bytes_accessed=16 * 2**20, transcendentals=0),
         name="merge",
-    )(prefix, valid, k_new, v_new, k_cache, v_cache)
+    )(prefix, valid, x_new, k_new, v_new, k_cache, v_cache)
 
 
 def solution(mesh):
@@ -600,8 +607,8 @@
         flat = (n_req, -1, head_dim)
         k_flat, v_flat = k_cache.reshape(flat), v_cache.reshape(flat)
         o, k_new, v_new, w_o_full = front(n_tp, mesh.shape["dp"], x_rows, g_attn, prefix, valid, freq, b_q, b_k, b_v, w_q, w_k, w_v, w_o, k_flat, v_flat)
-        k_out, v_out = merge(prefix, valid, k_new, v_new, k_flat, v_flat)
         out = tail(n_tp, o, x_rows, g_mlp, w_o_full, w_gate.T, w_up.T, w_down)
+        out, k_out, v_out = merge(prefix, valid, out, k_new, v_new, k_flat, v_flat)
         return out, k_out.reshape(k_cache.shape), v_out.reshape(v_cache.shape)
 
     in_specs = (row_spec, cache_spec, cache_spec, req_spec, req_spec, rep_spec, col_spec, bias_spec, col_spec, bias_spec, col_spec, bias_spec, down_spec, rep_spec, col_spec, col_spec, down_spec)

time: 195 us -> 195 us (level)
  no operation moved by 1% of the time
where the time goes in v7:
time: 195 us; the launch traced here: 194 us
  Pallas kernels  194 us (99%)
    pallas_call x1, Pallas kernels, tail(): pl.pallas_call(functools.partial(tail_kernel, n_tp), out_shape=jax.ShapeD...  96.2 us
    pallas_call x1, Pallas kernels, front(): pl.pallas_call(functools.partial(front_kernel, n_tp, n_dp), out_shape=[ja...  89.8 us
    pallas_call x1, Pallas kernels, merge(): pl.pallas_call(merge_kernel, out_shape=[jax.ShapeDtypeStruct(x_new.shape,...  7.56 us

profile of v7, /device:TPU:28, one launch (start us, length us, event | category | flops | bytes accessed | tf_op | source)
XLA Modules:
  0.0 194.4 jit_solution(17520959575997221918)
XLA Ops:
  0.6 89.8 %front.1 = (bf16[2,64,2048]{2,1,0:T(8,128)(2,1)}, bf16[2,1024,128]{2,1,0:T(8,128)(2,1)}, bf16[2,1024,128]{2,1,0:T(8,128)(2,1)}, bf16[2048,2048]{1,0:T(8,128)(2,1)}) custom-call(s32[2]{0:T(128)} %p_ref.3, s32[2]{0:T(128)} %c_ref.3, bf16[2,64,2048]{2,1,0:T(8,128)(2,1)} %x_ref.3, bf16[2048]{0:T(1024)(128)(2,1)} %g_ref.2, f32[1,128]{1,0:T(1,128)} %constant.2.clone.f_ref, ...), custom_call_target="tpu_custom_call" | custom-call | flops 17179869184 | bytes 20971520 | tf_op jit(solution)/shard_map/front/pallas_call | solution.py:501
  90.4 96.2 %tail.1.x_hbm = bf16[2,64,2048]{2,1,0:T(8,128)(2,1)} custom-call(bf16[2,64,2048]{2,1,0:T(8,128)(2,1)} %get-tuple-element.10.o_all, bf16[2,64,2048]{2,1,0:T(8,128)(2,1)} %x_ref.3, bf16[2048]{0:T(1024)(128)(2,1)} %g_ref.3, bf16[2048,2048]{1,0:T(8,128)(2,1)} %get-tuple-element.11.wo_hbm, bf16[688,2048]{1,0:T(8,128)(2,1)} %bitcast.16, ...), custom_call_target="tpu_custom_call" | custom-call | flops 17314086912 | bytes 20971520 | tf_op jit(solution)/shard_map/tail/pallas_call | solution.py:158
  186.6 7.6 %merge.1 = (bf16[2,64,2048]{2,1,0:T(8,128)(2,1)}, bf16[2,8192,128]{2,1,0:T(8,128)(2,1)}, bf16[2,8192,128]{2,1,0:T(8,128)(2,1)}) custom-call(s32[2]{0:T(128)} %p_ref.3, s32[2]{0:T(128)} %c_ref.3, bf16[2,64,2048]{2,1,0:T(8,128)(2,1)} %tail.1.x_hbm, bf16[2,1024,128]{2,1,0:T(8,128)(2,1)} %get-tuple-element.12.kn_hbm, ...), custom_call_target="tpu_custom_call" | custom-call | flops 1000000 | bytes 16777216 | tf_op jit(solution)/shard_map/merge/pallas_call | solution.py:572
